TPU v7x, 32 devices: a whole 2x2x4 slice. The times are simulated.
32 devices in a mesh: batch: 8 (over z, y), vocab: 4 (over x, core).
Axes of the slice: x: 2, y: 2, z: 4, core: 2. Of those that a mesh axis runs over, the one named last changes fastest.
Arguments:
- hidden: bfloat16 [4096, 3584], P(('batch', 'vocab')), may hold values from -6 to 6
- head_weight: bfloat16 [3072, 3584], P('vocab', 'batch'), may hold values from -0.3125 to 0.3125
- targets: int32 [4096], P(('batch', 'vocab')), may hold values from 0 to 3071
- valid_mask: int32 [4096], P(('batch', 'vocab')), may hold values 0 or 1
Outputs:
- head_grad: float32 [3072, 3584], P('vocab', 'batch')
- hidden_grad: float32 [4096, 3584], P(('batch', 'vocab'))
- mean_loss: float32 [], replicated
All inputs are finite; a program needn't handle non-finite values. No bound on the sum of `valid_mask` on one device may be relied on, other than what follows from the above.
Results may differ from a plain program's by a relative error of at most 0.0019.
Values may be sent and summed in bfloat16 or wider, within the bound.
A program may use at most 128 MiB of HBM per device.

v0:
```python
import functools

import jax
import jax.numpy as jnp
from jax import lax
from jax.experimental import pallas as pl
from jax.experimental.pallas import tpu as pltpu
from jax.sharding import PartitionSpec as P

softcap = 30.0
MESH = pl.DeviceIdType.MESH
f32, bf16 = jnp.float32, jnp.bfloat16


def chunk_of(length, most):
    return max(s for s in range(16, most + 1, 16) if length % s == 0)


def kernel(sizes, h_in, w_in, code_in, head_out, hid_out, loss_out, h_all, w_all, code_got, code_all,
           logits, delta, stat_own, stat_all, loss_own, loss_all, grad, grad_send, r_in,
           part, core_in, x_out, x_in, y_out, y_in, far_own, far_in, *sems):
    nz, ny, nx, nv = sizes
    (own_sem, hs, hf, hd, hr, ws_up, ws_dn, ws_y, wr, cs, cr, ss, sr, ls, lr,
     rs, rr, ds, dr, xs, xr, ys, yr, fs, fr) = sems
    nb = nz * ny
    rows, width = h_in.shape
    cols, half = w_in.shape[1:]
    group = ny * nv
    tokens = rows * group
    entries = ny * half
    b, v = lax.axis_index("batch"), lax.axis_index("vocab")
    z, y = lax.div(b, ny), lax.rem(b, ny)
    x, core = lax.div(v, 2), lax.rem(v, 2)
    other = x * 2 + 1 - core
    me = y * nv + v

    def at(bb, vv):
        return {"batch": bb, "vocab": vv}

    def copy(src, dst, send, recv, bb, vv):
        return pltpu.make_async_remote_copy(
            src_ref=src, dst_ref=dst, send_sem=send, recv_sem=recv, device_id=at(bb, vv), device_id_type=MESH)

    def hrow(i):
        return pl.ds(pl.multiple_of(i * rows, 16), rows)

    def wrow(i):
        return pl.ds(pl.multiple_of(i * cols, 16), cols)

    def turn_y(k):
        return lax.rem(y + k, ny)

    def turn_x(k):
        return lax.rem(x + k, nx)

    peers = [(k, j) for k in range(ny) for j in range(nv) if k or j]

    def peer(n):
        k, j = peers[n]
        return z * ny + turn_y(k), lax.rem(v + j, nv), turn_y(k) * nv + lax.rem(v + j, nv)

    barrier = pltpu.get_barrier_semaphore()
    for k in range(1, nb):
        pl.semaphore_signal(barrier, inc=1, device_id=at(lax.rem(b + k, nb), v), device_id_type=MESH)
    met = [n for n in range(len(peers)) if peers[n][1]]
    for n in met:
        bb, vv, _ = peer(n)
        pl.semaphore_signal(barrier, inc=1, device_id=at(bb, vv), device_id_type=MESH)
    pl.semaphore_wait(barrier, nb - 1 + len(met))

    def w_z(zz, yy, up, own=False):
        i = zz * ny + yy
        dst = w_all.at[wrow(i)]
        sem = (ws_up if up else ws_dn).at[i]
        return copy(w_in.at[y] if own else dst, dst, sem, wr.at[i], b + ny if up else b - ny, v)

    def w_y(k):
        return copy(w_in.at[turn_y(k)], w_all.at[wrow(b)], ws_y.at[k - 1], wr.at[b], z * ny + turn_y(k), v)

    def w_got(zz, yy):
        w_z(zz, yy, True).wait_recv()

    has_up, has_down = z + 1 < nz, z >= 1

    def h_send(n_src, sem, bb, vv, own=False):
        dst = h_all.at[hrow(n_src)]
        return copy(h_in if own else dst, dst, sem, hr.at[n_src], bb, vv)

    def h_x(k):
        return h_send(me, hs.at[k - 1], b, turn_x(k) * 2 + core, True)

    def h_y(k):
        return h_send(me, hs.at[nx + k - 1], z * ny + turn_y(k), v, True)

    def h_xy(kx, ky):
        return h_send(y * nv + turn_x(kx) * 2 + core, hf.at[kx, ky], z * ny + turn_y(ky), v)

    def h_yx(kx, ky):
        return h_send(turn_y(ky) * nv + v, hf.at[kx, ky], b, turn_x(kx) * 2 + core)

    def h_core(kx, ky):
        i = turn_y(ky) * nv + turn_x(kx) * 2 + core
        return h_send(i, hd.at[kx, ky], b, other, kx == 0 and ky == 0)

    def h_got(kx, ky, cc):
        i = turn_y(ky) * nv + turn_x(kx) * 2 + cc
        h_send(i, hd.at[kx, ky], b, other).wait_recv()

    def code_copy(n):
        bb, vv, _ = peer(n)
        return copy(code_in, code_got.at[me], cs.at[n], cr.at[me], bb, vv)

    for k in range(1, ny):
        w_y(k).start()
    pl.when(has_up)(lambda: w_z(z, y, True, True).start())
    pl.when(has_down)(lambda: w_z(z, y, False, True).start())
    for k in range(1, nx):
        h_x(k).start()
    for k in range(1, ny):
        h_y(k).start()
    for n in range(len(peers)):
        code_copy(n).start()
    h_core(0, 0).start()
    local = [
        pltpu.make_async_copy(w_in.at[y], w_all.at[wrow(b)], own_sem.at[0]),
        pltpu.make_async_copy(h_in, h_all.at[hrow(me)], own_sem.at[1]),
    ]
    for one in local:
        one.start()

    for k in range(1, ny):
        w_got(z, turn_y(k))
        pl.when(has_up)(lambda: w_z(z, turn_y(k), True).start())
        pl.when(has_down)(lambda: w_z(z, turn_y(k), False).start())

    def h_pass():
        for kx in range(1, nx):
            h_got(kx, 0, core)
            for ky in range(1, ny):
                pl.when(core == 0)(lambda: h_xy(kx, ky).start())
            h_core(kx, 0).start()
        for ky in range(1, ny):
            h_got(0, ky, core)
            for kx in range(1, nx):
                pl.when(core == 1)(lambda: h_yx(kx, ky).start())
            h_core(0, ky).start()

    def h_rest():
        for kx in range(1, nx):
            for ky in range(1, ny):
                h_got(kx, ky, core)
                h_core(kx, ky).start()

    for k in range(1, nz):
        for j in range(ny):
            yy = turn_y(j)

            @pl.when(z - k >= 0)
            def _():
                w_got(z - k, yy)
                pl.when(has_up)(lambda: w_z(z - k, yy, True).start())

            @pl.when(z + k < nz)
            def _():
                w_got(z + k, yy)
                pl.when(has_down)(lambda: w_z(z + k, yy, False).start())
        if k == 1:
            h_pass()
        if k == min(2, nz - 1):
            h_rest()

    for one in local:
        one.wait()
    for kx in range(nx):
        for ky in range(ny):
            h_got(kx, ky, 1 - core)
    code_got[me] = code_in[...]
    for n in range(len(peers)):
        bb, vv, i = peer(n)
        copy(code_in, code_got.at[i], cs.at[n], cr.at[i], bb, vv).wait_recv()
    for i in range(group):
        code_all[i * rows:(i + 1) * rows, :] = jnp.transpose(jnp.concatenate([code_got[i]] * 16, axis=0))

    step = chunk_of(tokens, 256)
    lanes = lax.broadcasted_iota(jnp.int32, (step, 128), 1)
    first = v * entries + y * half

    def span_of(n):
        return pl.ds(pl.multiple_of(n * step, step), step)

    def hits(n):
        ids = lax.broadcasted_iota(jnp.int32, (step, half), 1) + first
        return ids == code_all[span_of(n), 0:1].astype(jnp.int32)

    for n in range(tokens // step):
        span = pl.ds(n * step, step)
        scores = jnp.dot(h_all[span, :], w_all[...], preferred_element_type=f32)
        capped = softcap * jnp.tanh(scores * (1.0 / softcap))
        logits[span, :] = capped
        total = jnp.sum(jnp.exp(capped), axis=1, keepdims=True)
        hit_sum = jnp.sum(jnp.where(hits(n), capped, 0.0), axis=1, keepdims=True)
        turned = jnp.transpose(jnp.where(lax.rem(lanes, 8) < 4, total, hit_sum))
        stat_own[:, n * step:(n + 1) * step] = turned[0:8]

    def stat_copy(n):
        bb, vv, _ = peer(n)
        return copy(stat_own, stat_all.at[me], ss.at[n], sr.at[me], bb, vv)

    for n in range(len(peers)):
        stat_copy(n).start()
    for n in range(len(peers)):
        bb, vv, i = peer(n)
        copy(stat_own, stat_all.at[i], ss.at[n], sr.at[i], bb, vv).wait_recv()
    stats = stat_own[...]
    for n in range(len(peers)):
        stats = stats + stat_all[peer(n)[2]]

    loss = jnp.zeros((1, 1), f32)
    for n in range(tokens // step):
        span = pl.ds(n * step, step)
        weight = (code_all[span, 0:1] >= 0).astype(f32)
        back = jnp.transpose(jnp.concatenate([stats[:, n * step:(n + 1) * step]] * 16, axis=0))
        partition, target_logit = back[:, 0:1], back[:, 4:5]
        loss = loss + jnp.sum(weight * (jnp.log(partition) - target_logit), axis=0, keepdims=True)
        capped = logits[span, :]
        slope = 1.0 - (capped * (1.0 / softcap)) ** 2
        delta[span, :] = ((jnp.exp(capped) * (weight / partition) - jnp.where(hits(n), weight, 0.0)) * slope
                          ).astype(bf16)
    loss_own[...] = jnp.broadcast_to(loss, loss_own.shape)

    def loss_copy(k):
        return copy(loss_own, loss_all.at[b], ls.at[k - 1], lr.at[b], lax.rem(b + k, nb), v)

    def r_copy(zz, yy):
        i = zz * ny + yy
        return copy(grad_send.at[wrow(i)], r_in.at[z, y], rs.at[i], rr.at[b], i, v)

    def grad_share(span):
        return lax.dot_general(h_all[:, span], delta[...], (((0,), (0,)), ((), ())), preferred_element_type=f32)

    slab = ny * cols
    relay = nz == 4 and slab % 128 == 0
    turn = jnp.where(z * 2 >= nz, 1, nz - 1)
    order = [lax.rem(z + turn * k, nz) for k in range(1, nz)] + [z]
    at_end = (z == 0) | (z == nz - 1)
    far = jnp.where(z * 2 >= nz, 0, nz - 1)
    near = jnp.where(z * 2 >= nz, z - 1, z + 1)

    def far_copy(yy):
        return copy(grad_send.at[wrow(far * ny + yy)], far_in.at[yy], fs.at[yy], fr.at[yy], near * ny + y, v)

    def direct(zz):
        return jnp.logical_not(at_end & (zz == far))
    if slab % 128 == 0:
        mine = y * cols
        for n in range(nz):
            zz = order[n]
            span = pl.ds(pl.multiple_of(zz * slab, 128), slab)
            share = grad_share(span)
            held = relay and n == 1
            if n == nz - 1:
                grad[...] = share
            if held:
                @pl.when(jnp.logical_not(at_end))
                def _():
                    far_own[...] = share

                @pl.when(at_end)
                def _():
                    grad_send[span, :] = share.astype(bf16)
                    for k in range(ny):
                        r_copy(zz, turn_y(k)).start()
            else:
                grad_send[span, :] = share.astype(bf16)
                for k in range(ny):
                    yy = turn_y(k)
                    if relay and n == 0:
                        pl.when(at_end)(lambda: far_copy(yy).start())
                        pl.when(jnp.logical_not(at_end))(lambda: r_copy(zz, yy).start())
                    elif n < nz - 1 or k:
                        r_copy(zz, yy).start()
    else:
        mine = b * cols
        wide = chunk_of(width, 256)

        def grad_step(j, carry):
            span = pl.ds(pl.multiple_of(j * wide, wide), wide)
            share = grad_share(span)
            grad[span, :] = share
            grad_send[span, :] = share.astype(bf16)
            return carry

        lax.fori_loop(0, width // wide, grad_step, 0)
        for n in range(nz):
            for k in range(ny):
                if n < nz - 1 or k:
                    r_copy(order[n], turn_y(k)).start()
    for k in range(1, nb):
        loss_copy(k).start()

    wide = chunk_of(width, 256)

    def part_step(j, carry):
        span = pl.ds(pl.multiple_of(j * wide, wide), wide)
        part[:, span] = lax.dot_general(
            delta[...], w_all[span, :], (((1,), (1,)), ((), ())), preferred_element_type=f32)
        return carry

    lax.fori_loop(0, width // wide, part_step, 0)

    def core_copy(kx, ky):
        i = turn_y(ky) * nv + turn_x(kx) * 2 + 1 - core
        return copy(part.at[hrow(i)], core_in.at[kx, ky], ds.at[kx, ky], dr.at[kx, ky], b, other)

    def x_copy(kx, ky):
        return copy(x_out.at[kx - 1, ky], x_in.at[kx - 1, ky], xs.at[kx, ky], xr.at[kx, ky],
                    b, turn_x(kx) * 2 + core)

    def y_copy(ky):
        return copy(y_out.at[ky - 1], y_in.at[ky - 1], ys.at[ky], yr.at[ky], z * ny + turn_y(ky), v)

    ways = [(kx % nx, ky % ny) for kx in range(1, nx + 1) for ky in range(1, ny + 1)]
    for kx, ky in ways:
        core_copy(kx, ky).start()
    hstep = 16

    def over_rows(start, body):
        def one(r, carry):
            body(pl.ds(pl.multiple_of(r * hstep, hstep), hstep),
                 pl.ds(pl.multiple_of(start + r * hstep, hstep), hstep))
            return carry

        lax.fori_loop(0, rows // hstep, one, 0)

    def start_of(kx, ky):
        return (turn_y(ky) * nv + turn_x(kx) * 2 + core) * rows

    for kx, ky in ways:
        core_copy(kx, ky).wait_recv()

        def core_sum(span, here):
            both = part[here, :] + core_in[kx, ky, span, :]
            if kx:
                x_out[kx - 1, ky, span, :] = both.astype(bf16)
            else:
                part[here, :] = both

        over_rows(start_of(kx, ky), core_sum)
        if kx:
            x_copy(kx, ky).start()

    cstep = chunk_of(cols, 64)

    def over_cols(body):
        def one(r, carry):
            body(pl.multiple_of(r * cstep, 16))
            return carry

        lax.fori_loop(0, cols // cstep, one, 0)

    if relay:
        @pl.when(jnp.logical_not(at_end))
        def _():
            for k in range(ny):
                yy = turn_y(k)
                far_copy(yy).wait_recv()

                def far_sum(r):
                    here = pl.ds(pl.multiple_of(yy * cols + r, 16), cstep)
                    there = pl.ds(pl.multiple_of((far * ny + yy) * cols + r, 16), cstep)
                    grad_send[there, :] = (far_own[here, :] + far_in[yy, pl.ds(r, cstep), :].astype(f32)).astype(bf16)

                over_cols(far_sum)
                r_copy(far, yy).start()

    for ky in [k % ny for k in range(1, ny + 1)]:
        for kx in range(1, nx):
            x_copy(kx, ky).wait_recv()

        def x_sum(span, here):
            total = part[here, :]
            for kx in range(1, nx):
                total = total + x_in[kx - 1, ky, span, :].astype(f32)
            if ky:
                y_out[ky - 1, span, :] = total.astype(bf16)
            else:
                hid_out[span, :] = total

        over_rows(start_of(0, ky), x_sum)
        if ky:
            y_copy(ky).start()

    def r_got(zz, yy):
        i = zz * ny + yy
        copy(grad_send.at[wrow(i)], r_in.at[zz, yy], rs.at[i], rr.at[i], i, v).wait_recv()

    for k in range(1, ny):
        r_got(z, turn_y(k))

    def first_sum(r):
        head_out[y, pl.ds(r, cstep), :] = grad[pl.ds(pl.multiple_of(mine + r, 16), cstep), :]
        for k in range(1, ny):
            head_out[turn_y(k), pl.ds(r, cstep), :] = r_in[z, turn_y(k), pl.ds(r, cstep), :].astype(f32)

    over_cols(first_sum)
    hops = [jnp.where(z * 2 >= nz, lax.rem(z + nz - n, nz), lax.rem(z + n, nz)) for n in range(1, nz)]
    for n in range(1, nz):
        zz = hops[n - 1]
        if n == nz - 1:
            for ky in range(1, ny):
                y_copy(ky).wait_recv()

                def y_sum(span, here):
                    hid_out[span, :] += y_in[ky - 1, span, :].astype(f32)

                over_rows(0, y_sum)

        def more_sum(r):
            for k in range(ny):
                head_out[turn_y(k), pl.ds(r, cstep), :] += r_in[zz, turn_y(k), pl.ds(r, cstep), :].astype(f32)

        def arrived():
            for k in range(ny):
                r_got(zz, turn_y(k))
            over_cols(more_sum)

        if relay:
            pl.when(direct(zz))(arrived)
        else:
            arrived()

    losses = loss_own[...]
    for k in range(1, nb):
        i = lax.rem(b + k, nb)
        copy(loss_own, loss_all.at[i], ls.at[k - 1], lr.at[i], i, v).wait_recv()
        losses = losses + loss_all[i]
    loss_out[...] = losses * (1.0 / (tokens * nb))

    for j in range(ny):
        yy = turn_y(j)
        pl.when(has_up)(lambda: w_z(z, yy, True, j == 0).wait_send())
        pl.when(has_down)(lambda: w_z(z, yy, False, j == 0).wait_send())
        for k in range(1, nz):
            @pl.when(z - k >= 0)
            def _():
                pl.when(has_up)(lambda: w_z(z - k, yy, True).wait_send())

            @pl.when(z + k < nz)
            def _():
                pl.when(has_down)(lambda: w_z(z + k, yy, False).wait_send())
    for k in range(1, ny):
        w_y(k).wait_send()
        h_y(k).wait_send()
        y_copy(k).wait_send()
    for k in range(1, nx):
        h_x(k).wait_send()
        for ky in range(1, ny):
            pl.when(core == 0)(lambda: h_xy(k, ky).wait_send())
            pl.when(core == 1)(lambda: h_yx(k, ky).wait_send())
    for kx, ky in ways:
        h_core(kx, ky).wait_send()
        core_copy(kx, ky).wait_send()
        if kx:
            x_copy(kx, ky).wait_send()
    for n in range(len(peers)):
        code_copy(n).wait_send()
        stat_copy(n).wait_send()
    for k in range(1, nb):
        loss_copy(k).wait_send()
    for n in range(nz):
        for k in range(ny):
            yy = turn_y(k)
            if relay and n == 0:
                pl.when(at_end)(lambda: far_copy(yy).wait_send())
                pl.when(jnp.logical_not(at_end))(lambda: r_copy(order[n], yy).wait_send())
            elif n < nz - 1 or k:
                r_copy(order[n], yy).wait_send()


def local(nb, nv, hidden, head_weight, targets, valid_mask):
    nx = nv // 2
    ny = nx if nx <= 2 and nb % nx == 0 else 1
    nz = nb // ny
    rows, width = hidden.shape
    entries, cols = head_weight.shape
    half = entries // ny
    group = ny * nv
    tokens = rows * group
    code = jnp.broadcast_to(jnp.where(valid_mask != 0, targets, -1).astype(f32)[None, :], (8, rows))
    weight = jnp.transpose(head_weight.reshape(ny, half, cols), (0, 2, 1))
    vm = pltpu.VMEM
    dma = pltpu.SemaphoreType.DMA
    slab = ny * cols
    ly, lx = max(ny - 1, 1), max(nx - 1, 1)
    buffers = [
        vm((tokens, width), bf16), vm((width, half), bf16), vm((group, 8, rows), f32), vm((tokens, 128), f32),
        vm((tokens, half), f32), vm((tokens, half), bf16),
        vm((8, tokens), f32), vm((group, 8, tokens), f32), vm((8, 128), f32), vm((nb, 8, 128), f32),
        vm((slab if slab % 128 == 0 else width, half), f32), vm((width, half), bf16), vm((nz, ny, cols, half), bf16),
        vm((tokens, width), f32), vm((nx, ny, rows, width), f32),
        vm((lx, ny, rows, width), bf16), vm((lx, ny, rows, width), bf16),
        vm((ly, rows, width), bf16), vm((ly, rows, width), bf16),
        vm((slab if nz == 4 else 16, half), f32), vm((ny, cols if nz == 4 else 16, half), bf16),
    ]
    sems = [
        dma((2,)), dma((nx + ny,)), dma((nx, ny)), dma((nx, ny)), dma((group,)), dma((nb,)), dma((nb,)),
        dma((ly,)), dma((nb,)), dma((group,)), dma((group,)), dma((group,)), dma((group,)), dma((nb,)), dma((nb,)),
        dma((nb,)), dma((nb,)), dma((nx, ny)), dma((nx, ny)), dma((nx, ny)), dma((nx, ny)), dma((ny,)), dma((ny,)),
        dma((ny,)), dma((ny,)),
    ]
    whole = pl.BlockSpec(memory_space=vm)
    head_t, hidden_grad, loss = pl.pallas_call(
        functools.partial(kernel, (nz, ny, nx, nv)),
        out_shape=(
            jax.ShapeDtypeStruct((ny, cols, half), f32),
            jax.ShapeDtypeStruct((rows, width), f32),
            jax.ShapeDtypeStruct((8, 128), f32),
        ),
        in_specs=[whole] * 3,
        out_specs=(whole,) * 3,
        scratch_shapes=buffers + sems,
        compiler_params=pltpu.CompilerParams(
            collective_id=0, has_side_effects=True, vmem_limit_bytes=67043328),
    )(hidden, weight, code)
    return jnp.transpose(head_t, (0, 2, 1)).reshape(entries, cols), hidden_grad, loss[0, 0]


def solution(mesh):
    placed = (
        P(("batch", "vocab"), None),
        P("vocab", "batch"),
        P(("batch", "vocab")),
        P(("batch", "vocab")),
    )
    return jax.shard_map(
        functools.partial(local, mesh.shape["batch"], mesh.shape["vocab"]),
        mesh=mesh,
        in_specs=placed,
        out_specs=(P("vocab", "batch"), P(("batch", "vocab"), None), P()),
        check_vma=False,
    )
```

profile of v0, /device:TPU:0, one launch (start us, length us, event | category | flops | bytes accessed | tf_op | source)
XLA Modules:
  0.0 139.7 jit_solution(9742618913272940516)
XLA Ops:
  0.6 0.7 fusion
  1.3 0.6 broadcast_in_dim.11.code_in
  1.9 2.0 %copy.12 = bf16[56,2,8,384]{3,2,0,1:T(8,128)(2,1)} copy(bf16[56,2,8,384]{3,2,1,0:T(8,128)(2,1)} %bitcast.14) | data formatting | bytes 1376256 | tf_op jit(solution)/shard_map/reshape | solution.py:490
  3.9 130.7 %shard_map.67 = (f32[2,448,384]{2,1,0:T(8,128)}, f32[128,3584]{1,0:T(8,128)}, f32[8,128]{1,0:T(8,128)}) custom-call(bf16[128,3584]{1,0:T(8,128)(2,1)} %h_in.1, bf16[2,448,384]{2,1,0:T(8,128)(2,1)} %bitcast.11, f32[8,128]{1,0:T(8,128)} %broadcast_in_dim.11.code_in), custom_call_target="tpu_custom_call" | custom-call | tf_op jit(solution)/shard_map/pallas_call | solution.py:512
  134.7 0.0 copy-start
  134.7 1.3 slice.3
  136.0 2.5 %copy.10 = f32[2,56,8,384]{3,2,0,1:T(8,128)} copy(f32[2,56,8,384]{3,2,1,0:T(8,128)} %bitcast.13) | data formatting | bytes 2752512 | tf_op jit(solution)/shard_map/reshape | solution.py:525
  138.5 0.0 copy-done
  138.5 1.2 copy.14
Async XLA Ops:
  134.7 3.9 %copy-start = (f32[128,3584]{1,0:T(8,128)S(1)}, f32[128,3584]{1,0:T(8,128)}, u32[]{:S(2)}) copy-start(f32[128,3584]{1,0:T(8,128)} %get-tuple-element.13) | copy-start | bytes 5505028
where the time goes:
time: 140 us
  Pallas kernels  131 us (94%)
  local copies, waits for them, and re-layouts  7.68 us (5%)
    pallas_call x1, Pallas kernels, local(): pl.pallas_call(functools.partial(kernel, (nz, ny, nx, nv)), out_shape=(ja...  131 us

commit v1 on v0

--- a/solution.py
+++ b/solution.py
@@ -525,6 +525,617 @@
     return jnp.transpose(head_t, (0, 2, 1)).reshape(entries, cols), hidden_grad, loss[0, 0]
 
 
+def column_groups(width):
+    units = width // 256
+    sizes, left = [2], units - 2
+    while left > 6:
+        sizes.append(3)
+        left -= 3
+    while left > 0:
+        take = max(1, (left + 1) // 2)
+        sizes.append(take)
+        left -= take
+    starts = [sum(sizes[:n]) for n in range(len(sizes))]
+    return [(s, n) for s, n in zip(starts, sizes)]
+
+
+def plane_kernel(h_in, w_in, code_in, head_out, hid_out, loss_out, h_all, w_all, code_got, code_all,
+                 logits, expo, delta, stat_own, stat_all, loss_one, loss_two, loss_all, loss_zs,
+                 grad_own, held, grad_send, far_in, r_in, part, core_in, x_out, x_in, y_out, y_in, *sems):
+    (own_sem, hs, hf, hd, hr, w_up, w_dn, wr, wys, cs, cr, ss, sr, ls, lr, ms, mr,
+     es, er, rs, rr, fs, fr, ds, dr, xs, xr, ys, yr) = sems
+    nz, ny, nv = 4, 2, 4
+    nb = nz * ny
+    rows, width = h_in.shape
+    cols, half = w_in.shape[0], w_in.shape[1] // ny
+    piece = cols // 2
+    group = ny * nv
+    tokens = rows * group
+    slab = ny * cols
+    shift, lo = cols % 128, cols - cols % 128
+    win = -(-(cols + shift) // 128) * 128
+    b, v = lax.axis_index("batch"), lax.axis_index("vocab")
+    z, y = lax.div(b, ny), lax.rem(b, ny)
+    x, core = lax.div(v, 2), lax.rem(v, 2)
+    me = y * nv + v
+    low = z * 2 < nz
+    at_end = (z == 0) | (z == nz - 1)
+    inside = jnp.logical_not(at_end)
+
+    def flip(a, k):
+        return 1 - a if k else a
+
+    def copy(src, dst, send, recv, bb, vv):
+        return pltpu.make_async_remote_copy(
+            src_ref=src, dst_ref=dst, send_sem=send, recv_sem=recv,
+            device_id={"batch": bb, "vocab": vv}, device_id_type=MESH)
+
+    def hrow(i):
+        return pl.ds(pl.multiple_of(i * rows, 16), rows)
+
+    over_x, over_y, over_core = (1 - x) * 2 + core, z * ny + 1 - y, x * 2 + 1 - core
+    peers = [(ky, kx, kc) for ky in range(2) for kx in range(2) for kc in range(2) if ky or kx or kc]
+
+    def peer(n):
+        ky, kx, kc = peers[n]
+        yy, vv = flip(y, ky), flip(x, kx) * 2 + flip(core, kc)
+        return z * ny + yy, vv, yy * nv + vv
+
+    def z_peer(k):
+        return lax.rem(z + k, nz) * ny + y
+
+    barrier = pltpu.get_barrier_semaphore()
+    for k in range(1, nz):
+        pl.semaphore_signal(barrier, inc=1, device_id={"batch": z_peer(k), "vocab": v}, device_id_type=MESH)
+    for n in range(len(peers)):
+        bb, vv, _ = peer(n)
+        pl.semaphore_signal(barrier, inc=1, device_id={"batch": bb, "vocab": vv}, device_id_type=MESH)
+    pl.semaphore_wait(barrier, nz - 1 + len(peers))
+
+    def w_ref(i, h):
+        return w_all.at[pl.ds(pl.multiple_of(i * cols + h * piece, 16), piece)]
+
+    def w_mine(yy, h):
+        return w_in.at[pl.ds(h * piece, piece), pl.ds(pl.multiple_of(yy * half, 128), half)]
+
+    def w_z(i, h, up, own=False):
+        return copy(w_mine(y, h) if own else w_ref(i, h), w_ref(i, h), (w_up if up else w_dn).at[i, h],
+                    wr.at[i, h], b + ny if up else b - ny, v)
+
+    def w_pass(i, h, up):
+        return copy(w_ref(i, h), w_ref(i, h), w_up.at[i, h], wr.at[i, h], jnp.where(up, b + ny, b - ny), v)
+
+    def w_y(h):
+        return copy(w_mine(1 - y, h), w_ref(b, h), wys.at[h], wr.at[b, h], over_y, v)
+
+    def w_got(i, h):
+        copy(w_ref(i, h), w_ref(i, h), wys.at[h], wr.at[i, h], over_y, v).wait_recv()
+
+    has_up, has_down = z + 1 < nz, z >= 1
+    near = z + 1 - 2 * lax.rem(z, 2)
+    slabs = [z, near, jnp.where(low, 2, 1), jnp.where(low, 3, 0)]
+
+    def h_send(i, sem, bb, vv, own=False):
+        dst = h_all.at[hrow(i)]
+        return copy(h_in if own else dst, dst, sem, hr.at[i], bb, vv)
+
+    def h_x():
+        return h_send(me, hs.at[0], b, over_x, True)
+
+    def h_y():
+        return h_send(me, hs.at[1], over_y, v, True)
+
+    def h_xy():
+        return h_send(y * nv + over_x, hf.at[0], over_y, v)
+
+    def h_yx():
+        return h_send((1 - y) * nv + v, hf.at[0], b, over_x)
+
+    def h_core(kx, ky):
+        i = flip(y, ky) * nv + flip(x, kx) * 2 + core
+        return h_send(i, hd.at[kx, ky], b, over_core, kx == 0 and ky == 0)
+
+    def h_got(kx, ky, cc):
+        i = flip(y, ky) * nv + flip(x, kx) * 2 + cc
+        h_send(i, hd.at[kx, ky], b, over_core).wait_recv()
+
+    def code_copy(n):
+        bb, vv, _ = peer(n)
+        return copy(code_in, code_got.at[me], cs.at[n], cr.at[me], bb, vv)
+
+    for h in range(2):
+        w_y(h).start()
+    for h in range(2):
+        pl.when(has_up)(lambda: w_z(b, h, True, True).start())
+        pl.when(has_down)(lambda: w_z(b, h, False, True).start())
+    h_x().start()
+    h_y().start()
+    for n in range(len(peers)):
+        code_copy(n).start()
+    h_core(0, 0).start()
+    local = [pltpu.make_async_copy(w_mine(y, h), w_ref(b, h), own_sem.at[h]) for h in range(2)]
+    local.append(pltpu.make_async_copy(h_in, h_all.at[hrow(me)], own_sem.at[2]))
+    for one in local:
+        one.start()
+
+    for h in range(2):
+        i = z * ny + 1 - y
+        w_got(i, h)
+        pl.when(has_up)(lambda: w_z(i, h, True).start())
+        pl.when(has_down)(lambda: w_z(i, h, False).start())
+
+    def w_slab(zz, onward):
+        for k in range(ny):
+            for h in range(2):
+                i = zz * ny + flip(y, k)
+                w_got(i, h)
+                if onward:
+                    w_pass(i, h, zz < z).start()
+
+    @pl.when(at_end)
+    def _():
+        w_slab(slabs[1], False)
+
+    @pl.when(inside)
+    def _():
+        w_slab(slabs[1], True)
+        w_slab(slabs[2], True)
+
+    h_got(1, 0, core)
+    pl.when(core == 0)(lambda: h_xy().start())
+    h_core(1, 0).start()
+    h_got(0, 1, core)
+    pl.when(core == 1)(lambda: h_yx().start())
+    h_core(0, 1).start()
+
+    @pl.when(at_end)
+    def _():
+        w_slab(slabs[2], False)
+
+    @pl.when(inside)
+    def _():
+        w_slab(slabs[3], True)
+
+    for one in local:
+        one.wait()
+    code_got[me] = code_in[...]
+    for n in range(len(peers)):
+        bb, vv, i = peer(n)
+        copy(code_in, code_got.at[i], cs.at[n], cr.at[i], bb, vv).wait_recv()
+    for i in range(group):
+        code_all[i * rows:(i + 1) * rows, :] = jnp.transpose(jnp.concatenate([code_got[i]] * (rows // 8), axis=0))
+
+    h_got(1, 1, core)
+    h_core(1, 1).start()
+    for kx in range(2):
+        for ky in range(2):
+            h_got(kx, ky, 1 - core)
+
+    step = 2 * rows
+    steps = tokens // step
+    lines = lax.broadcasted_iota(jnp.int32, (8, rows), 0)
+
+    def scores(n, zz):
+        here = pl.ds(pl.multiple_of(zz * slab, 128), slab)
+        there = pl.ds(pl.multiple_of(zz * slab, 16), slab)
+        return jnp.dot(h_all[n * step:(n + 1) * step, here], w_all[there, :], preferred_element_type=f32)
+
+    for j in range(nz - 1):
+        for n in range(steps):
+            span = pl.ds(n * step, step)
+            if j:
+                logits[span, :] += scores(n, slabs[j])
+            else:
+                logits[span, :] = scores(n, slabs[j])
+
+    pl.when(at_end)(lambda: w_slab(slabs[3], False))
+
+    sums = jnp.zeros((8, rows), f32)
+    for n in range(steps):
+        span = pl.ds(n * step, step)
+        capped = softcap * jnp.tanh((logits[span, :] + scores(n, slabs[nz - 1])) * (1.0 / softcap))
+        raised = jnp.exp(capped)
+        logits[span, :] = capped
+        expo[span, :] = raised
+        total = jnp.broadcast_to(jnp.sum(raised, axis=1, keepdims=True), (step, 128))
+        for k in range(2):
+            turned = jnp.transpose(total[k * rows:(k + 1) * rows])
+            sums = jnp.where(lines == 2 * n + k, turned[0:8], sums)
+    stat_own[...] = sums
+
+    def stat_copy(n):
+        bb, vv, _ = peer(n)
+        return copy(stat_own, stat_all.at[me], ss.at[n], sr.at[me], bb, vv)
+
+    for n in range(len(peers)):
+        stat_copy(n).start()
+
+    ids = (lax.broadcasted_iota(jnp.int32, (step, half), 1) + (v * ny + y) * half).astype(f32)
+    hit_total = jnp.zeros((step, 1), f32)
+    for n in range(steps):
+        span = pl.ds(n * step, step)
+        capped = logits[span, :]
+        hit = ids == code_all[span, 0:1]
+        slope = 1.0 - (capped * (1.0 / softcap)) ** 2
+        expo[span, :] = expo[span, :] * slope
+        logits[span, :] = jnp.where(hit, slope, 0.0)
+        hit_total = hit_total + jnp.sum(jnp.where(hit, capped, 0.0), axis=1, keepdims=True)
+    hit_total = jnp.sum(hit_total, axis=0, keepdims=True)
+    code_rows = jnp.zeros((8, rows), f32)
+    for i in range(group):
+        code_rows = jnp.where(lines == i, code_got[i], code_rows)
+    weight = (code_rows >= 0).astype(f32)
+
+    stat_all[me] = sums
+    for n in range(len(peers)):
+        bb, vv, i = peer(n)
+        copy(stat_own, stat_all.at[i], ss.at[n], sr.at[i], bb, vv).wait_recv()
+    partition = stat_all[0]
+    for i in range(1, group):
+        partition = partition + stat_all[i]
+    scale = weight / partition
+
+    def delta_copy(n):
+        span = pl.ds(n * step, step)
+        return copy(delta.at[0, span], delta.at[1, span], es.at[n], er.at[n], over_y, v)
+
+    for n in range(steps):
+        for k in range(2):
+            i = 2 * n + k
+            span = pl.ds(i * rows, rows)
+            by_row = jnp.transpose(jnp.broadcast_to(scale[i:i + 1, :], (rows, rows)))
+            factor = jnp.concatenate([by_row] * (half // rows), axis=1)
+            delta[0, span, :] = (expo[span, :] * factor - logits[span, :]).astype(bf16)
+        delta_copy(n).start()
+
+    share_loss = jnp.sum(weight * jnp.log(partition), axis=1, keepdims=True)
+    loss = jnp.sum(share_loss, axis=0, keepdims=True) * (1.0 / group) - hit_total
+    loss_one[...] = jnp.broadcast_to(loss, loss_one.shape)
+
+    def loss_copy(n):
+        bb, vv, _ = peer(n)
+        return copy(loss_one, loss_all.at[me], ls.at[n], lr.at[me], bb, vv)
+
+    near_end = jnp.where(low, 1, 2)
+    far = jnp.where(low, nz - 1, 0)
+    targets = [jnp.where(lax.rem(z, 2) == 0, nz - 1, 0), jnp.where(low, 2, 1),
+               jnp.where(at_end, near_end, far), z]
+    top = y * shift
+
+    def grad_share(zz, r):
+        here = pl.ds(pl.multiple_of(zz * slab + y * lo, 128), win)
+        return lax.dot_general(h_all[:, here], delta[r], (((0,), (0,)), ((), ())), preferred_element_type=f32)
+
+    def sent(k, r):
+        return grad_send.at[k, r, pl.ds(pl.multiple_of(top, 16), cols)]
+
+    def r_copy(k, r):
+        return copy(sent(k, r), r_in.at[z, r], rs.at[k, r], rr.at[z, r], targets[k] * ny + y, v)
+
+    def far_copy(r):
+        return copy(sent(0, r), far_in.at[r], fs.at[r], fr.at[r], near_end * ny + y, v)
+
+    def head_piece(k, r):
+        share = grad_share(targets[k], r)
+        if k == nz - 1:
+            grad_own[r] = share
+        elif k == 2:
+            @pl.when(at_end)
+            def _():
+                grad_send[k, r] = share.astype(bf16)
+                r_copy(k, r).start()
+
+            @pl.when(inside)
+            def _():
+                held[r] = share
+        else:
+            grad_send[k, r] = share.astype(bf16)
+            if k == 0:
+                pl.when(at_end)(lambda: far_copy(r).start())
+                pl.when(inside)(lambda: r_copy(k, r).start())
+            else:
+                r_copy(k, r).start()
+
+    cstep = chunk_of(cols, 64)
+
+    def over_cols(body):
+        def one(n, carry):
+            body(pl.multiple_of(n * cstep, 16))
+            return carry
+
+        lax.fori_loop(0, cols // cstep, one, 0)
+
+    def relay(r):
+        @pl.when(inside)
+        def _():
+            far_copy(r).wait_recv()
+
+            def add(n):
+                here = pl.ds(pl.multiple_of(top + n, 16), cstep)
+                grad_send[2, r, here, :] = (held[r, here, :] + far_in[r, pl.ds(n, cstep), :].astype(f32)).astype(bf16)
+
+            over_cols(add)
+            r_copy(2, r).start()
+
+    groups = column_groups(width)
+    blocks = [(1, 1), (1, 0), (0, 1), (0, 0)]
+    unit = width // (width // 256)
+
+    def span_of(g):
+        first, n = groups[g]
+        return pl.ds(first * unit, n * unit)
+
+    def block(kx, ky, cc):
+        return flip(y, ky) * nv + flip(x, kx) * 2 + cc
+
+    def core_copy(g, kx, ky):
+        return copy(part.at[hrow(block(kx, ky, 1 - core)), span_of(g)], core_in.at[kx, ky, :, span_of(g)],
+                    ds.at[g, kx, ky], dr.at[g, kx, ky], b, over_core)
+
+    def x_copy(g, ky):
+        return copy(x_out.at[ky, :, span_of(g)], x_in.at[ky, :, span_of(g)], xs.at[g, ky], xr.at[g, ky], b, over_x)
+
+    def y_copy(g):
+        return copy(y_out.at[:, span_of(g)], y_in.at[:, span_of(g)], ys.at[g], yr.at[g], over_y, v)
+
+    def part_group(g):
+        first, n = groups[g]
+
+        def one(j, carry):
+            span = pl.ds(pl.multiple_of(j * unit, 128), unit)
+            part[:, span] = lax.dot_general(
+                delta[0], w_all[span, :], (((1,), (1,)), ((), ())), preferred_element_type=f32)
+            return carry
+
+        lax.fori_loop(first, first + n, one, 0)
+        for kx, ky in blocks:
+            core_copy(g, kx, ky).start()
+
+    hstep = 16
+
+    def over_rows(body):
+        def one(n, carry):
+            body(pl.multiple_of(n * hstep, hstep))
+            return carry
+
+        lax.fori_loop(0, rows // hstep, one, 0)
+
+    def core_sum(g):
+        span = span_of(g)
+        for kx, ky in blocks:
+            core_copy(g, kx, ky).wait_recv()
+            start = block(kx, ky, core) * rows
+
+            def add(n):
+                here = pl.ds(pl.multiple_of(start + n, hstep), hstep)
+                both = part[here, span] + core_in[kx, ky, pl.ds(n, hstep), span]
+                if kx:
+                    x_out[ky, pl.ds(n, hstep), span] = both.astype(bf16)
+                else:
+                    part[here, span] = both
+
+            over_rows(add)
+            if kx:
+                x_copy(g, ky).start()
+
+    def x_sum(g):
+        span = span_of(g)
+        for ky in (1, 0):
+            x_copy(g, ky).wait_recv()
+            start = block(0, ky, core) * rows
+
+            def add(n):
+                here = pl.ds(pl.multiple_of(start + n, hstep), hstep)
+                total = part[here, span] + x_in[ky, pl.ds(n, hstep), span].astype(f32)
+                if ky:
+                    y_out[pl.ds(n, hstep), span] = total.astype(bf16)
+                else:
+                    hid_out[pl.ds(n, hstep), span] = total
+
+            over_rows(add)
+            if ky:
+                y_copy(g).start()
+
+    def y_sum(g):
+        span = span_of(g)
+        y_copy(g).wait_recv()
+
+        def add(n):
+            here = pl.ds(n, hstep)
+            hid_out[here, span] += y_in[here, span].astype(f32)
+
+        over_rows(add)
+
+    count = len(groups)
+    head_piece(0, 0)
+    part_group(0)
+    head_piece(1, 0)
+    part_group(1)
+    for n in range(len(peers)):
+        loss_copy(n).start()
+    core_sum(0)
+    head_piece(2, 0)
+    for g in range(2, count):
+        part_group(g)
+        core_sum(g - 1)
+        if g == 3:
+            relay(0)
+    core_sum(count - 1)
+    head_piece(3, 0)
+
+    loss_all[me] = loss_one[...]
+    for n in range(len(peers)):
+        bb, vv, i = peer(n)
+        copy(loss_one, loss_all.at[i], ls.at[n], lr.at[i], bb, vv).wait_recv()
+    losses = loss_all[0]
+    for i in range(1, group):
+        losses = losses + loss_all[i]
+    loss_two[...] = losses
+
+    def plane_copy(k):
+        return copy(loss_two, loss_zs.at[z], ms.at[k - 1], mr.at[z], z_peer(k), v)
+
+    for k in range(1, nz):
+        plane_copy(k).start()
+
+    x_sum(0)
+    for n in range(steps):
+        delta_copy(n).wait_recv()
+    for k in range(nz):
+        head_piece(k, 1)
+        if k == 1:
+            x_sum(1)
+    x_sum(2)
+    relay(1)
+    for g in range(3, count):
+        x_sum(g)
+        y_sum(g - 3)
+
+    def r_got(zz, r):
+        copy(r_in.at[zz, r], r_in.at[zz, r], rs.at[0, r], rr.at[zz, r], z_peer(1), v).wait_recv()
+
+    def lanes(r):
+        return pl.ds(pl.multiple_of(flip(y, r) * half, 128), half)
+
+    sources = [near, jnp.where(low, 2, 1), far]
+
+    def head_sum(r):
+        for k in range(2):
+            r_got(sources[k], r)
+
+        def add(n):
+            here = pl.ds(n, cstep)
+            total = grad_own[r, pl.ds(pl.multiple_of(top + n, 16), cstep), :]
+            for k in range(2):
+                total = total + r_in[sources[k], r, here, :].astype(f32)
+            head_out[here, lanes(r)] = total
+
+        over_cols(add)
+
+        @pl.when(inside)
+        def _():
+            r_got(sources[2], r)
+
+            def last(n):
+                here = pl.ds(n, cstep)
+                head_out[here, lanes(r)] += r_in[sources[2], r, here, :].astype(f32)
+
+            over_cols(last)
+
+    head_sum(0)
+    y_sum(count - 3)
+    y_sum(count - 2)
+    loss_zs[z] = loss_two[...]
+    for k in range(1, nz):
+        i = lax.rem(z + k, nz)
+        copy(loss_two, loss_zs.at[i], ms.at[k - 1], mr.at[i], z_peer(k), v).wait_recv()
+    losses = loss_zs[0]
+    for i in range(1, nz):
+        losses = losses + loss_zs[i]
+    loss_out[...] = losses * (1.0 / (tokens * nz))
+    y_sum(count - 1)
+    head_sum(1)
+
+    for h in range(2):
+        w_y(h).wait_send()
+        pl.when(has_up)(lambda: w_z(b, h, True, True).wait_send())
+        pl.when(has_down)(lambda: w_z(b, h, False, True).wait_send())
+        pl.when(has_up)(lambda: w_z(z * ny + 1 - y, h, True).wait_send())
+        pl.when(has_down)(lambda: w_z(z * ny + 1 - y, h, False).wait_send())
+
+    @pl.when(inside)
+    def _():
+        for j in range(1, nz):
+            for k in range(ny):
+                for h in range(2):
+                    w_pass(slabs[j] * ny + flip(y, k), h, slabs[j] < z).wait_send()
+
+    h_x().wait_send()
+    h_y().wait_send()
+    pl.when(core == 0)(lambda: h_xy().wait_send())
+    pl.when(core == 1)(lambda: h_yx().wait_send())
+    for kx, ky in blocks:
+        h_core(kx, ky).wait_send()
+    for n in range(len(peers)):
+        code_copy(n).wait_send()
+        stat_copy(n).wait_send()
+        loss_copy(n).wait_send()
+    for k in range(1, nz):
+        plane_copy(k).wait_send()
+    for n in range(steps):
+        delta_copy(n).wait_send()
+    for r in range(2):
+        pl.when(at_end)(lambda: far_copy(r).wait_send())
+        pl.when(inside)(lambda: r_copy(0, r).wait_send())
+        r_copy(1, r).wait_send()
+        r_copy(2, r).wait_send()
+    for g in range(count):
+        for kx, ky in blocks:
+            core_copy(g, kx, ky).wait_send()
+        for ky in range(2):
+            x_copy(g, ky).wait_send()
+        y_copy(g).wait_send()
+
+
+def plane_local(hidden, head_weight, targets, valid_mask):
+    nz, ny, nv = 4, 2, 4
+    rows, width = hidden.shape
+    entries, cols = head_weight.shape
+    half = entries // ny
+    group = ny * nv
+    tokens = rows * group
+    shift = cols % 128
+    win = -(-(cols + shift) // 128) * 128
+    code = jnp.broadcast_to(jnp.where(valid_mask != 0, targets, -1).astype(f32)[None, :], (8, rows))
+    vm = pltpu.VMEM
+    dma = pltpu.SemaphoreType.DMA
+    count = len(column_groups(width))
+    line = vm((8, rows), f32)
+    buffers = [
+        vm((tokens, width), bf16), vm((width, half), bf16), vm((group, 8, rows), f32), vm((tokens, 128), f32),
+        vm((tokens, half), f32), vm((tokens, half), f32), vm((2, tokens, half), bf16),
+        line, vm((group, 8, rows), f32), line, line, vm((group, 8, rows), f32), vm((nz, 8, rows), f32),
+        vm((2, win, half), f32), vm((2, win, half), f32), vm((3, 2, win, half), bf16),
+        vm((2, cols, half), bf16), vm((nz, 2, cols, half), bf16),
+        vm((tokens, width), f32), vm((2, 2, rows, width), f32),
+        vm((2, rows, width), bf16), vm((2, rows, width), bf16), vm((rows, width), bf16), vm((rows, width), bf16),
+    ]
+    sems = [
+        dma((3,)), dma((2,)), dma((1,)), dma((2, 2)), dma((group,)), dma((8, 2)), dma((8, 2)), dma((8, 2)), dma((2,)),
+        dma((7,)), dma((group,)), dma((7,)), dma((group,)), dma((7,)), dma((group,)), dma((3,)), dma((nz,)),
+        dma((4,)), dma((4,)), dma((3, 2)), dma((nz, 2)), dma((2,)), dma((2,)),
+        dma((count, 2, 2)), dma((count, 2, 2)), dma((count, 2)), dma((count, 2)), dma((count,)), dma((count,)),
+    ]
+    whole = pl.BlockSpec(memory_space=vm)
+    head_t, hidden_grad, loss = pl.pallas_call(
+        plane_kernel,
+        out_shape=(
+            jax.ShapeDtypeStruct((cols, entries), f32),
+            jax.ShapeDtypeStruct((rows, width), f32),
+            jax.ShapeDtypeStruct((8, rows), f32),
+        ),
+        in_specs=[whole] * 3,
+        out_specs=(whole,) * 3,
+        scratch_shapes=buffers + sems,
+        compiler_params=pltpu.CompilerParams(
+            collective_id=1, has_side_effects=True, vmem_limit_bytes=67043328),
+    )(hidden, jnp.transpose(head_weight), code)
+    return jnp.transpose(head_t), hidden_grad, loss[0, 0]
+
+
+def in_planes(nb, nv, hidden, head_weight, targets, valid_mask):
+    rows, width = hidden.shape
+    entries, cols = head_weight.shape
+    fits = nb == 8 and nv == 4 and rows == 128 and width % 256 == 0 and width >= 2048
+    return fits and entries % 256 == 0 and cols % 32 == 0 and (2 * cols) % 128 == 0
+
+
+def device(nb, nv, *arrays):
+    if in_planes(nb, nv, *arrays):
+        return plane_local(*arrays)
+    return local(nb, nv, *arrays)
+
+
 def solution(mesh):
     placed = (
         P(("batch", "vocab"), None),
@@ -533,7 +1144,7 @@
         P(("batch", "vocab")),
     )
     return jax.shard_map(
-        functools.partial(local, mesh.shape["batch"], mesh.shape["vocab"]),
+        functools.partial(device, mesh.shape["batch"], mesh.shape["vocab"]),
         mesh=mesh,
         in_specs=placed,
         out_specs=(P("vocab", "batch"), P(("batch", "vocab"), None), P()),

time: 140 us -> 118 us (0.84)
  Pallas kernels: 131 us -> 111 us
  local copies, waits for them, and re-layouts: 7.68 us -> 5.66 us
    pallas_call x1, Pallas kernels: 131 us -> 111 us  [plane_local(): pl.pallas_call(plane_kernel, out_shape=(jax.ShapeDtypeStruct((cols, entri...]
    reshape x2 -> x0, local copies, waits for them, and re-layouts: 4.53 us -> none  [the longest x1 2.52 us: local(): jnp.transpose(head_t, (0, 2, 1)).reshape(entries, cols)]
    unnamed x3 -> x4, local copies, waits for them, and re-layouts: 1.23 us -> 3.74 us
where the time goes in v1:
time: 118 us
  Pallas kernels  111 us (94%)
  local copies, waits for them, and re-layouts  5.66 us (5%)
    pallas_call x1, Pallas kernels, plane_local(): pl.pallas_call(plane_kernel, out_shape=(jax.ShapeDtypeStruct((cols, entri...  111 us
    unnamed x4, local copies, waits for them, and re-layouts  3.74 us

profile of v1, /device:TPU:0, one launch (start us, length us, event | category | flops | bytes accessed | tf_op | source)
XLA Modules:
  0.0 117.7 jit_solution(13357842665882511029)
XLA Ops:
  0.6 0.7 fusion
  1.3 0.6 broadcast_in_dim.11.code_in
  1.9 110.7 %shard_map.67 = (f32[448,768]{1,0:T(8,128)}, f32[128,3584]{1,0:T(8,128)}, f32[8,128]{1,0:T(8,128)}) custom-call(bf16[128,3584]{1,0:T(8,128)(2,1)} %h_in.1, bf16[448,768]{1,0:T(8,128)(2,1)} %bitcast.4, f32[8,128]{1,0:T(8,128)} %broadcast_in_dim.11.code_in), custom_call_target="tpu_custom_call" | custom-call | tf_op jit(solution)/shard_map/pallas_call | solution.py:1110
  112.6 0.0 copy-start
  112.6 1.3 %slice.3 = f32[1,1]{1,0:T(1,128)} slice(f32[8,128]{1,0:T(8,128)} %get-tuple-element.8), slice={[0:1], [0:1]} | slice | bytes 8 | tf_op jit(solution)/shard_map/slice | solution.py:1123
  114.0 2.5 %copy.9 = f32[768,448]{0,1:T(8,128)} copy(f32[768,448]{0,1:T(8,128)} %bitcast.3) | data formatting | bytes 2752512
  116.5 0.0 copy-done
  116.5 1.2 %copy.10 = f32[128,3584]{1,0:T(8,128)} copy(f32[128,3584]{1,0:T(8,128)S(1)} %copy-done) | data formatting | bytes 3670016
Async XLA Ops:
  112.6 3.8 %copy-start = (f32[128,3584]{1,0:T(8,128)S(1)}, f32[128,3584]{1,0:T(8,128)}, u32[]{:S(2)}) copy-start(f32[128,3584]{1,0:T(8,128)} %get-tuple-element.13) | copy-start | bytes 5505028

commit v2 on v1

--- a/solution.py
+++ b/solution.py
@@ -539,7 +539,8 @@
     return [(s, n) for s, n in zip(starts, sizes)]
 
 
-def plane_kernel(h_in, w_in, code_in, head_out, hid_out, loss_out, h_all, w_all, code_got, code_all,
+def plane_kernel(h_in, w_in, ids_in, mask_in, head_out, hid_out, loss_out, h_all, w_all, w_over, ids_own, mask_own,
+                 code_own, code_got, code_all,
                  logits, expo, delta, stat_own, stat_all, loss_one, loss_two, loss_all, loss_zs,
                  grad_own, held, grad_send, far_in, r_in, part, core_in, x_out, x_in, y_out, y_in, *sems):
     (own_sem, hs, hf, hd, hr, w_up, w_dn, wr, wys, cs, cr, ss, sr, ls, lr, ms, mr,
@@ -590,23 +591,35 @@
     for n in range(len(peers)):
         bb, vv, _ = peer(n)
         pl.semaphore_signal(barrier, inc=1, device_id={"batch": bb, "vocab": vv}, device_id_type=MESH)
+    first = pl.ds(pl.multiple_of(y * half, 128), half)
+    second = pl.ds(pl.multiple_of((1 - y) * half, 128), half)
+    local = [
+        pltpu.make_async_copy(w_in.at[:, second], w_over, own_sem.at[0]),
+        pltpu.make_async_copy(w_in.at[:, first], w_all.at[pl.ds(pl.multiple_of(b * cols, 16), cols)], own_sem.at[1]),
+        pltpu.make_async_copy(ids_in, ids_own, own_sem.at[2]),
+        pltpu.make_async_copy(mask_in, mask_own, own_sem.at[3]),
+        pltpu.make_async_copy(h_in, h_all.at[hrow(me)], own_sem.at[4]),
+    ]
+    for one in local:
+        one.start()
+    for one in local:
+        one.wait()
+    code = jnp.where(mask_own[...] != 0, ids_own[...], -1).astype(f32)
+    code_own[...] = jnp.broadcast_to(code, code_own.shape)
     pl.semaphore_wait(barrier, nz - 1 + len(peers))
 
     def w_ref(i, h):
         return w_all.at[pl.ds(pl.multiple_of(i * cols + h * piece, 16), piece)]
 
-    def w_mine(yy, h):
-        return w_in.at[pl.ds(h * piece, piece), pl.ds(pl.multiple_of(yy * half, 128), half)]
-
-    def w_z(i, h, up, own=False):
-        return copy(w_mine(y, h) if own else w_ref(i, h), w_ref(i, h), (w_up if up else w_dn).at[i, h],
+    def w_z(i, h, up):
+        return copy(w_ref(i, h), w_ref(i, h), (w_up if up else w_dn).at[i, h],
                     wr.at[i, h], b + ny if up else b - ny, v)
 
     def w_pass(i, h, up):
         return copy(w_ref(i, h), w_ref(i, h), w_up.at[i, h], wr.at[i, h], jnp.where(up, b + ny, b - ny), v)
 
     def w_y(h):
-        return copy(w_mine(1 - y, h), w_ref(b, h), wys.at[h], wr.at[b, h], over_y, v)
+        return copy(w_over.at[pl.ds(h * piece, piece)], w_ref(b, h), wys.at[h], wr.at[b, h], over_y, v)
 
     def w_got(i, h):
         copy(w_ref(i, h), w_ref(i, h), wys.at[h], wr.at[i, h], over_y, v).wait_recv()
@@ -615,15 +628,14 @@
     near = z + 1 - 2 * lax.rem(z, 2)
     slabs = [z, near, jnp.where(low, 2, 1), jnp.where(low, 3, 0)]
 
-    def h_send(i, sem, bb, vv, own=False):
-        dst = h_all.at[hrow(i)]
-        return copy(h_in if own else dst, dst, sem, hr.at[i], bb, vv)
+    def h_send(i, sem, bb, vv):
+        return copy(h_all.at[hrow(i)], h_all.at[hrow(i)], sem, hr.at[i], bb, vv)
 
     def h_x():
-        return h_send(me, hs.at[0], b, over_x, True)
+        return h_send(me, hs.at[0], b, over_x)
 
     def h_y():
-        return h_send(me, hs.at[1], over_y, v, True)
+        return h_send(me, hs.at[1], over_y, v)
 
     def h_xy():
         return h_send(y * nv + over_x, hf.at[0], over_y, v)
@@ -633,7 +645,7 @@
 
     def h_core(kx, ky):
         i = flip(y, ky) * nv + flip(x, kx) * 2 + core
-        return h_send(i, hd.at[kx, ky], b, over_core, kx == 0 and ky == 0)
+        return h_send(i, hd.at[kx, ky], b, over_core)
 
     def h_got(kx, ky, cc):
         i = flip(y, ky) * nv + flip(x, kx) * 2 + cc
@@ -641,31 +653,26 @@
 
     def code_copy(n):
         bb, vv, _ = peer(n)
-        return copy(code_in, code_got.at[me], cs.at[n], cr.at[me], bb, vv)
+        return copy(code_own, code_got.at[me], cs.at[n], cr.at[me], bb, vv)
 
     for h in range(2):
         w_y(h).start()
     for h in range(2):
-        pl.when(has_up)(lambda: w_z(b, h, True, True).start())
-        pl.when(has_down)(lambda: w_z(b, h, False, True).start())
+        pl.when(has_up)(lambda: w_z(b, h, True).start())
+        pl.when(has_down)(lambda: w_z(b, h, False).start())
     h_x().start()
     h_y().start()
     for n in range(len(peers)):
         code_copy(n).start()
     h_core(0, 0).start()
-    local = [pltpu.make_async_copy(w_mine(y, h), w_ref(b, h), own_sem.at[h]) for h in range(2)]
-    local.append(pltpu.make_async_copy(h_in, h_all.at[hrow(me)], own_sem.at[2]))
-    for one in local:
-        one.start()
-
     for h in range(2):
         i = z * ny + 1 - y
         w_got(i, h)
         pl.when(has_up)(lambda: w_z(i, h, True).start())
         pl.when(has_down)(lambda: w_z(i, h, False).start())
 
-    def w_slab(zz, onward):
-        for k in range(ny):
+    def w_slab(zz, onward, which=(0, 1)):
+        for k in which:
             for h in range(2):
                 i = zz * ny + flip(y, k)
                 w_got(i, h)
@@ -696,12 +703,10 @@
     def _():
         w_slab(slabs[3], True)
 
-    for one in local:
-        one.wait()
-    code_got[me] = code_in[...]
+    code_got[me] = code_own[...]
     for n in range(len(peers)):
         bb, vv, i = peer(n)
-        copy(code_in, code_got.at[i], cs.at[n], cr.at[i], bb, vv).wait_recv()
+        copy(code_own, code_got.at[i], cs.at[n], cr.at[i], bb, vv).wait_recv()
     for i in range(group):
         code_all[i * rows:(i + 1) * rows, :] = jnp.transpose(jnp.concatenate([code_got[i]] * (rows // 8), axis=0))
 
@@ -715,9 +720,9 @@
     steps = tokens // step
     lines = lax.broadcasted_iota(jnp.int32, (8, rows), 0)
 
-    def scores(n, zz):
-        here = pl.ds(pl.multiple_of(zz * slab, 128), slab)
-        there = pl.ds(pl.multiple_of(zz * slab, 16), slab)
+    def scores(n, zz, at=0, wide=slab):
+        here = pl.ds(pl.multiple_of(zz * slab + at, 128), wide)
+        there = pl.ds(pl.multiple_of(zz * slab + at, 16), wide)
         return jnp.dot(h_all[n * step:(n + 1) * step, here], w_all[there, :], preferred_element_type=f32)
 
     for j in range(nz - 1):
@@ -728,12 +733,16 @@
             else:
                 logits[span, :] = scores(n, slabs[j])
 
-    pl.when(at_end)(lambda: w_slab(slabs[3], False))
+    early = lo
+    pl.when(at_end)(lambda: w_slab(slabs[3], False, (0,)))
+    for n in range(steps):
+        logits[n * step:(n + 1) * step, :] += scores(n, slabs[3], y * (slab - early), early)
+    pl.when(at_end)(lambda: w_slab(slabs[3], False, (1,)))
 
     sums = jnp.zeros((8, rows), f32)
     for n in range(steps):
         span = pl.ds(n * step, step)
-        capped = softcap * jnp.tanh((logits[span, :] + scores(n, slabs[nz - 1])) * (1.0 / softcap))
+        capped = softcap * jnp.tanh((logits[span, :] + scores(n, slabs[3], (1 - y) * early, slab - early)) * (1.0 / softcap))
         raised = jnp.exp(capped)
         logits[span, :] = capped
         expo[span, :] = raised
@@ -1038,8 +1047,8 @@
 
     for h in range(2):
         w_y(h).wait_send()
-        pl.when(has_up)(lambda: w_z(b, h, True, True).wait_send())
-        pl.when(has_down)(lambda: w_z(b, h, False, True).wait_send())
+        pl.when(has_up)(lambda: w_z(b, h, True).wait_send())
+        pl.when(has_down)(lambda: w_z(b, h, False).wait_send())
         pl.when(has_up)(lambda: w_z(z * ny + 1 - y, h, True).wait_send())
         pl.when(has_down)(lambda: w_z(z * ny + 1 - y, h, False).wait_send())
 
@@ -1086,13 +1095,13 @@
     tokens = rows * group
     shift = cols % 128
     win = -(-(cols + shift) // 128) * 128
-    code = jnp.broadcast_to(jnp.where(valid_mask != 0, targets, -1).astype(f32)[None, :], (8, rows))
     vm = pltpu.VMEM
     dma = pltpu.SemaphoreType.DMA
     count = len(column_groups(width))
     line = vm((8, rows), f32)
     buffers = [
-        vm((tokens, width), bf16), vm((width, half), bf16), vm((group, 8, rows), f32), vm((tokens, 128), f32),
+        vm((tokens, width), bf16), vm((width, half), bf16), vm((cols, half), bf16),
+        vm((1, rows), jnp.int32), vm((1, rows), jnp.int32), line, vm((group, 8, rows), f32), vm((tokens, 128), f32),
         vm((tokens, half), f32), vm((tokens, half), f32), vm((2, tokens, half), bf16),
         line, vm((group, 8, rows), f32), line, line, vm((group, 8, rows), f32), vm((nz, 8, rows), f32),
         vm((2, win, half), f32), vm((2, win, half), f32), vm((3, 2, win, half), bf16),
@@ -1101,7 +1110,7 @@
         vm((2, rows, width), bf16), vm((2, rows, width), bf16), vm((rows, width), bf16), vm((rows, width), bf16),
     ]
     sems = [
-        dma((3,)), dma((2,)), dma((1,)), dma((2, 2)), dma((group,)), dma((8, 2)), dma((8, 2)), dma((8, 2)), dma((2,)),
+        dma((5,)), dma((2,)), dma((1,)), dma((2, 2)), dma((group,)), dma((8, 2)), dma((8, 2)), dma((8, 2)), dma((2,)),
         dma((7,)), dma((group,)), dma((7,)), dma((group,)), dma((7,)), dma((group,)), dma((3,)), dma((nz,)),
         dma((4,)), dma((4,)), dma((3, 2)), dma((nz, 2)), dma((2,)), dma((2,)),
         dma((count, 2, 2)), dma((count, 2, 2)), dma((count, 2)), dma((count, 2)), dma((count,)), dma((count,)),
@@ -1110,16 +1119,16 @@
     head_t, hidden_grad, loss = pl.pallas_call(
         plane_kernel,
         out_shape=(
-            jax.ShapeDtypeStruct((cols, entries), f32),
-            jax.ShapeDtypeStruct((rows, width), f32),
-            jax.ShapeDtypeStruct((8, rows), f32),
+            vm((cols, entries), f32),
+            vm((rows, width), f32),
+            vm((8, rows), f32),
         ),
-        in_specs=[whole] * 3,
+        in_specs=[pl.BlockSpec(memory_space=pl.ANY)] * 4,
         out_specs=(whole,) * 3,
         scratch_shapes=buffers + sems,
         compiler_params=pltpu.CompilerParams(
-            collective_id=1, has_side_effects=True, vmem_limit_bytes=67043328),
-    )(hidden, jnp.transpose(head_weight), code)
+            collective_id=1, has_side_effects=True, vmem_limit_bytes=58 * 1024 * 1024),
+    )(hidden, jnp.transpose(head_weight), targets[None, :], valid_mask[None, :])
     return jnp.transpose(head_t), hidden_grad, loss[0, 0]
 
 

time: 118 us -> 111 us (0.941)
  Pallas kernels: 111 us -> 108 us
  local copies, waits for them, and re-layouts: 5.66 us -> 2.82 us
    pallas_call x1, Pallas kernels: 111 us -> 108 us  [plane_local(): pl.pallas_call(plane_kernel, out_shape=(vm((cols, entries), f32), vm((row...]
    unnamed x4 -> x2, local copies, waits for them, and re-layouts: 3.74 us -> 2.31 us
where the time goes in v2:
time: 111 us
  Pallas kernels  108 us (97%)
  local copies, waits for them, and re-layouts  2.82 us (3%)
    pallas_call x1, Pallas kernels, plane_local(): pl.pallas_call(plane_kernel, out_shape=(vm((cols, entries), f32), vm((row...  108 us
    unnamed x2, local copies, waits for them, and re-layouts  2.31 us

profile of v2, /device:TPU:0, one launch (start us, length us, event | category | flops | bytes accessed | tf_op | source)
XLA Modules:
  0.0 111.1 jit_solution(2360483538815864111)
XLA Ops:
  0.6 107.6 %shard_map.67 = (f32[448,768]{1,0:T(8,128)S(1)}, f32[128,3584]{1,0:T(8,128)S(1)}, f32[8,128]{1,0:T(8,128)S(1)}) custom-call(bf16[128,3584]{1,0:T(8,128)(2,1)} %h_in.1, bf16[448,768]{1,0:T(8,128)(2,1)} %bitcast.6, s32[1,128]{1,0:T(1,128)} %bitcast.7, s32[1,128]{1,0:T(1,128)} %bitcast.8), custom_call_target="tpu_custom_call" | custom-call | tf_op jit(solution)/shard_map/pallas_call | solution.py:1119
  108.3 0.5 slice.3
  108.8 1.1 copy.9
  109.9 1.2 %copy.10 = f32[128,3584]{1,0:T(8,128)} copy(f32[128,3584]{1,0:T(8,128)S(1)} %get-tuple-element.10) | data formatting | bytes 3670016

commit v3 on v2

--- a/solution.py
+++ b/solution.py
@@ -527,14 +527,11 @@
 
 def column_groups(width):
     units = width // 256
-    sizes, left = [2], units - 2
-    while left > 6:
-        sizes.append(3)
-        left -= 3
+    sizes, left = [1, 2], units - 5
     while left > 0:
-        take = max(1, (left + 1) // 2)
-        sizes.append(take)
-        left -= take
+        sizes.append(min(3, left))
+        left -= sizes[-1]
+    sizes += [1, 1]
     starts = [sum(sizes[:n]) for n in range(len(sizes))]
     return [(s, n) for s, n in zip(starts, sizes)]
 
@@ -543,8 +540,8 @@
                  code_own, code_got, code_all,
                  logits, expo, delta, stat_own, stat_all, loss_one, loss_two, loss_all, loss_zs,
                  grad_own, held, grad_send, far_in, r_in, part, core_in, x_out, x_in, y_out, y_in, *sems):
-    (own_sem, hs, hf, hd, hr, w_up, w_dn, wr, wys, cs, cr, ss, sr, ls, lr, ms, mr,
-     es, er, rs, rr, fs, fr, ds, dr, xs, xr, ys, yr) = sems
+    (own_sem, hs, hr, ws, wr, wys, cs, cr, ss, sr, ls, lr, ms, mr,
+     es, er, rs, rr, nr, fr, ds, dr, xs, xr, ys, yr) = sems
     nz, ny, nv = 4, 2, 4
     nb = nz * ny
     rows, width = h_in.shape
@@ -612,48 +609,48 @@
         return w_all.at[pl.ds(pl.multiple_of(i * cols + h * piece, 16), piece)]
 
     def w_z(i, h, up):
-        return copy(w_ref(i, h), w_ref(i, h), (w_up if up else w_dn).at[i, h],
+        return copy(w_ref(i, h), w_ref(i, h), ws.at[0 if up else 1],
                     wr.at[i, h], b + ny if up else b - ny, v)
 
     def w_pass(i, h, up):
-        return copy(w_ref(i, h), w_ref(i, h), w_up.at[i, h], wr.at[i, h], jnp.where(up, b + ny, b - ny), v)
+        return copy(w_ref(i, h), w_ref(i, h), ws.at[jnp.where(up, 0, 1)], wr.at[i, h], jnp.where(up, b + ny, b - ny), v)
 
     def w_y(h):
-        return copy(w_over.at[pl.ds(h * piece, piece)], w_ref(b, h), wys.at[h], wr.at[b, h], over_y, v)
+        return copy(w_over.at[pl.ds(h * piece, piece)], w_ref(b, h), wys.at[0], wr.at[b, h], over_y, v)
 
     def w_got(i, h):
-        copy(w_ref(i, h), w_ref(i, h), wys.at[h], wr.at[i, h], over_y, v).wait_recv()
+        copy(w_ref(i, h), w_ref(i, h), wys.at[0], wr.at[i, h], over_y, v).wait_recv()
 
     has_up, has_down = z + 1 < nz, z >= 1
     near = z + 1 - 2 * lax.rem(z, 2)
     slabs = [z, near, jnp.where(low, 2, 1), jnp.where(low, 3, 0)]
 
-    def h_send(i, sem, bb, vv):
-        return copy(h_all.at[hrow(i)], h_all.at[hrow(i)], sem, hr.at[i], bb, vv)
+    def h_send(i, bb, vv):
+        return copy(h_all.at[hrow(i)], h_all.at[hrow(i)], hs.at[0], hr.at[i], bb, vv)
 
     def h_x():
-        return h_send(me, hs.at[0], b, over_x)
+        return h_send(me, b, over_x)
 
     def h_y():
-        return h_send(me, hs.at[1], over_y, v)
+        return h_send(me, over_y, v)
 
     def h_xy():
-        return h_send(y * nv + over_x, hf.at[0], over_y, v)
+        return h_send(y * nv + over_x, over_y, v)
 
     def h_yx():
-        return h_send((1 - y) * nv + v, hf.at[0], b, over_x)
+        return h_send((1 - y) * nv + v, b, over_x)
 
     def h_core(kx, ky):
         i = flip(y, ky) * nv + flip(x, kx) * 2 + core
-        return h_send(i, hd.at[kx, ky], b, over_core)
+        return h_send(i, b, over_core)
 
     def h_got(kx, ky, cc):
         i = flip(y, ky) * nv + flip(x, kx) * 2 + cc
-        h_send(i, hd.at[kx, ky], b, over_core).wait_recv()
+        h_send(i, b, over_core).wait_recv()
 
     def code_copy(n):
         bb, vv, _ = peer(n)
-        return copy(code_own, code_got.at[me], cs.at[n], cr.at[me], bb, vv)
+        return copy(code_own, code_got.at[me], cs.at[0], cr.at[0], bb, vv)
 
     for h in range(2):
         w_y(h).start()
@@ -704,9 +701,8 @@
         w_slab(slabs[3], True)
 
     code_got[me] = code_own[...]
-    for n in range(len(peers)):
-        bb, vv, i = peer(n)
-        copy(code_own, code_got.at[i], cs.at[n], cr.at[i], bb, vv).wait_recv()
+    others = pl.ds(0, group - 1)
+    copy(code_got.at[others], code_got.at[others], cs.at[0], cr.at[0], b, over_x).wait_recv()
     for i in range(group):
         code_all[i * rows:(i + 1) * rows, :] = jnp.transpose(jnp.concatenate([code_got[i]] * (rows // 8), axis=0))
 
@@ -754,7 +750,7 @@
 
     def stat_copy(n):
         bb, vv, _ = peer(n)
-        return copy(stat_own, stat_all.at[me], ss.at[n], sr.at[me], bb, vv)
+        return copy(stat_own, stat_all.at[me], ss.at[0], sr.at[0], bb, vv)
 
     for n in range(len(peers)):
         stat_copy(n).start()
@@ -770,15 +766,21 @@
         logits[span, :] = jnp.where(hit, slope, 0.0)
         hit_total = hit_total + jnp.sum(jnp.where(hit, capped, 0.0), axis=1, keepdims=True)
     hit_total = jnp.sum(hit_total, axis=0, keepdims=True)
+    loss_one[...] = jnp.broadcast_to(hit_total, loss_one.shape)
+
+    def hit_copy(n):
+        bb, vv, _ = peer(n)
+        return copy(loss_one, loss_all.at[me], ls.at[0], lr.at[0], bb, vv)
+
+    for n in range(len(peers)):
+        hit_copy(n).start()
     code_rows = jnp.zeros((8, rows), f32)
     for i in range(group):
         code_rows = jnp.where(lines == i, code_got[i], code_rows)
     weight = (code_rows >= 0).astype(f32)
 
     stat_all[me] = sums
-    for n in range(len(peers)):
-        bb, vv, i = peer(n)
-        copy(stat_own, stat_all.at[i], ss.at[n], sr.at[i], bb, vv).wait_recv()
+    copy(stat_all.at[others], stat_all.at[others], ss.at[0], sr.at[0], b, over_x).wait_recv()
     partition = stat_all[0]
     for i in range(1, group):
         partition = partition + stat_all[i]
@@ -786,7 +788,7 @@
 
     def delta_copy(n):
         span = pl.ds(n * step, step)
-        return copy(delta.at[0, span], delta.at[1, span], es.at[n], er.at[n], over_y, v)
+        return copy(delta.at[0, span], delta.at[1, span], es.at[0], er.at[0], over_y, v)
 
     for n in range(steps):
         for k in range(2):
@@ -797,50 +799,75 @@
             delta[0, span, :] = (expo[span, :] * factor - logits[span, :]).astype(bf16)
         delta_copy(n).start()
 
-    share_loss = jnp.sum(weight * jnp.log(partition), axis=1, keepdims=True)
-    loss = jnp.sum(share_loss, axis=0, keepdims=True) * (1.0 / group) - hit_total
-    loss_one[...] = jnp.broadcast_to(loss, loss_one.shape)
-
-    def loss_copy(n):
-        bb, vv, _ = peer(n)
-        return copy(loss_one, loss_all.at[me], ls.at[n], lr.at[me], bb, vv)
-
     near_end = jnp.where(low, 1, 2)
     far = jnp.where(low, nz - 1, 0)
-    targets = [jnp.where(lax.rem(z, 2) == 0, nz - 1, 0), jnp.where(low, 2, 1),
-               jnp.where(at_end, near_end, far), z]
+    across = jnp.where(low, 2, 1)
+    targets = [jnp.where(at_end, far, across), jnp.where(at_end, across, near), jnp.where(at_end, near_end, far), z]
     top = y * shift
 
-    def grad_share(zz, r):
+    def grad_share(zz, r, first, wide):
         here = pl.ds(pl.multiple_of(zz * slab + y * lo, 128), win)
-        return lax.dot_general(h_all[:, here], delta[r], (((0,), (0,)), ((), ())), preferred_element_type=f32)
+        return lax.dot_general(h_all[:, here], delta[r, :, first:first + wide], (((0,), (0,)), ((), ())), preferred_element_type=f32)
 
     def sent(k, r):
         return grad_send.at[k, r, pl.ds(pl.multiple_of(top, 16), cols)]
 
     def r_copy(k, r):
-        return copy(sent(k, r), r_in.at[z, r], rs.at[k, r], rr.at[z, r], targets[k] * ny + y, v)
+        return copy(sent(k, r), r_in.at[z, r], rs.at[0], rr.at[z, r], targets[k] * ny + y, v)
 
     def far_copy(r):
-        return copy(sent(0, r), far_in.at[r], fs.at[r], fr.at[r], near_end * ny + y, v)
+        return copy(sent(0, r), far_in.at[r], rs.at[0], fr.at[r], near_end * ny + y, v)
+
+    bounds = [(0, 128), (128, half - 128)]
+
+    def far_part(n):
+        here = pl.ds(*bounds[n])
+        return copy(grad_send.at[0, 0, pl.ds(pl.multiple_of(top, 16), cols), here], far_in.at[0, :, here],
+                    rs.at[0], fr.at[(0, 2)[n]], near_end * ny + y, v)
+
+    def cross_copy():
+        return copy(sent(1, 1), far_in.at[2], rs.at[0], fr.at[3], near_end * ny + y, v)
+
+    def near_copy(r, h):
+        src = grad_send.at[2, r, pl.ds(pl.multiple_of(top + h * piece, 16), piece)]
+        return copy(src, r_in.at[z, r, pl.ds(h * piece, piece)], rs.at[0], nr.at[r, h], near_end * ny + y, v)
+
+    def first_piece():
+        for n in range(2):
+            first, wide = bounds[n]
+            grad_send[0, 0, :, first:first + wide] = grad_share(targets[0], 0, first, wide).astype(bf16)
+            pl.when(at_end)(lambda: far_part(n).start())
+        pl.when(inside)(lambda: r_copy(0, 0).start())
 
     def head_piece(k, r):
-        share = grad_share(targets[k], r)
+        share = grad_share(targets[k], r, 0, half)
         if k == nz - 1:
             grad_own[r] = share
         elif k == 2:
             @pl.when(at_end)
             def _():
                 grad_send[k, r] = share.astype(bf16)
-                r_copy(k, r).start()
+                near_copy(r, 0).start()
+                if r:
+                    near_copy(0, 1).start()
+                    near_copy(1, 1).start()
 
             @pl.when(inside)
             def _():
                 held[r] = share
+        elif k == 0:
+            @pl.when(at_end)
+            def _():
+                grad_send[k, r] = share.astype(bf16)
+                far_copy(r).start()
+
+            @pl.when(inside)
+            def _():
+                held[2] = share
         else:
             grad_send[k, r] = share.astype(bf16)
-            if k == 0:
-                pl.when(at_end)(lambda: far_copy(r).start())
+            if r:
+                pl.when(at_end)(lambda: cross_copy().start())
                 pl.when(inside)(lambda: r_copy(k, r).start())
             else:
                 r_copy(k, r).start()
@@ -854,17 +881,24 @@
 
         lax.fori_loop(0, cols // cstep, one, 0)
 
-    def relay(r):
+    def relay(k, r, slot):
         @pl.when(inside)
         def _():
-            far_copy(r).wait_recv()
+            if r == 0:
+                for n in range(2):
+                    far_part(n).wait_recv()
+            elif k:
+                far_copy(r).wait_recv()
+            else:
+                cross_copy().wait_recv()
 
             def add(n):
                 here = pl.ds(pl.multiple_of(top + n, 16), cstep)
-                grad_send[2, r, here, :] = (held[r, here, :] + far_in[r, pl.ds(n, cstep), :].astype(f32)).astype(bf16)
+                there = pl.ds(n, cstep)
+                grad_send[k, r, here, :] = (held[slot, here, :] + far_in[slot, there, :].astype(f32)).astype(bf16)
 
             over_cols(add)
-            r_copy(2, r).start()
+            r_copy(k, r).start()
 
     groups = column_groups(width)
     blocks = [(1, 1), (1, 0), (0, 1), (0, 0)]
@@ -874,31 +908,41 @@
         first, n = groups[g]
         return pl.ds(first * unit, n * unit)
 
-    def block(kx, ky, cc):
+    y_first = (3,)
+
+    def block(g, one, two, cc):
+        kx, ky = (two, one) if g in y_first else (one, two)
         return flip(y, ky) * nv + flip(x, kx) * 2 + cc
 
-    def core_copy(g, kx, ky):
-        return copy(part.at[hrow(block(kx, ky, 1 - core)), span_of(g)], core_in.at[kx, ky, :, span_of(g)],
-                    ds.at[g, kx, ky], dr.at[g, kx, ky], b, over_core)
-
-    def x_copy(g, ky):
-        return copy(x_out.at[ky, :, span_of(g)], x_in.at[ky, :, span_of(g)], xs.at[g, ky], xr.at[g, ky], b, over_x)
-
-    def y_copy(g):
-        return copy(y_out.at[:, span_of(g)], y_in.at[:, span_of(g)], ys.at[g], yr.at[g], over_y, v)
+    def core_copy(g, one, two):
+        return copy(part.at[hrow(block(g, one, two, 1 - core)), span_of(g)], core_in.at[one, two, :, span_of(g)],
+                    ds.at[0], dr.at[g], b, over_core)
+
+    def over_one(g):
+        return (over_y, v) if g in y_first else (b, over_x)
+
+    def over_two(g):
+        return (b, over_x) if g in y_first else (over_y, v)
+
+    def one_copy(g, two):
+        return copy(x_out.at[two, :, span_of(g)], x_in.at[two, :, span_of(g)], xs.at[0], xr.at[g, two],
+                    *over_one(g))
+
+    def two_copy(g):
+        return copy(y_out.at[:, span_of(g)], y_in.at[:, span_of(g)], ys.at[0], yr.at[g], *over_two(g))
 
     def part_group(g):
         first, n = groups[g]
 
-        def one(j, carry):
+        def columns(j, carry):
             span = pl.ds(pl.multiple_of(j * unit, 128), unit)
             part[:, span] = lax.dot_general(
                 delta[0], w_all[span, :], (((1,), (1,)), ((), ())), preferred_element_type=f32)
             return carry
 
-        lax.fori_loop(first, first + n, one, 0)
-        for kx, ky in blocks:
-            core_copy(g, kx, ky).start()
+        lax.fori_loop(first, first + n, columns, 0)
+        for one, two in blocks:
+            core_copy(g, one, two).start()
 
     hstep = 16
 
@@ -911,43 +955,44 @@
 
     def core_sum(g):
         span = span_of(g)
-        for kx, ky in blocks:
-            core_copy(g, kx, ky).wait_recv()
-            start = block(kx, ky, core) * rows
+        landed = core_in.at[:, :, :, span]
+        copy(landed, landed, ds.at[0], dr.at[g], b, over_core).wait_recv()
+        for one, two in blocks:
+            start = block(g, one, two, core) * rows
 
             def add(n):
                 here = pl.ds(pl.multiple_of(start + n, hstep), hstep)
-                both = part[here, span] + core_in[kx, ky, pl.ds(n, hstep), span]
-                if kx:
-                    x_out[ky, pl.ds(n, hstep), span] = both.astype(bf16)
+                both = part[here, span] + core_in[one, two, pl.ds(n, hstep), span]
+                if one:
+                    x_out[two, pl.ds(n, hstep), span] = both.astype(bf16)
                 else:
                     part[here, span] = both
 
             over_rows(add)
-            if kx:
-                x_copy(g, ky).start()
-
-    def x_sum(g):
+            if one:
+                one_copy(g, two).start()
+
+    def one_sum(g):
         span = span_of(g)
-        for ky in (1, 0):
-            x_copy(g, ky).wait_recv()
-            start = block(0, ky, core) * rows
+        for two in (1, 0):
+            one_copy(g, two).wait_recv()
+            start = block(g, 0, two, core) * rows
 
             def add(n):
                 here = pl.ds(pl.multiple_of(start + n, hstep), hstep)
-                total = part[here, span] + x_in[ky, pl.ds(n, hstep), span].astype(f32)
-                if ky:
+                total = part[here, span] + x_in[two, pl.ds(n, hstep), span].astype(f32)
+                if two:
                     y_out[pl.ds(n, hstep), span] = total.astype(bf16)
                 else:
                     hid_out[pl.ds(n, hstep), span] = total
 
             over_rows(add)
-            if ky:
-                y_copy(g).start()
-
-    def y_sum(g):
+            if two:
+                two_copy(g).start()
+
+    def two_sum(g):
         span = span_of(g)
-        y_copy(g).wait_recv()
+        two_copy(g).wait_recv()
 
         def add(n):
             here = pl.ds(n, hstep)
@@ -956,52 +1001,74 @@
         over_rows(add)
 
     count = len(groups)
-    head_piece(0, 0)
+
+    def plane_copy(k):
+        return copy(loss_two, loss_zs.at[z], ms.at[0], mr.at[0], z_peer(k), v)
+
+    def plane_loss():
+        loss_all[me] = loss_one[...]
+        copy(loss_all.at[others], loss_all.at[others], ls.at[0], lr.at[0], b, over_x).wait_recv()
+        hits = loss_all[0]
+        for i in range(1, group):
+            hits = hits + loss_all[i]
+        logs = jnp.sum(weight * jnp.log(partition), axis=1, keepdims=True)
+        loss_two[...] = jnp.broadcast_to(jnp.sum(logs, axis=0, keepdims=True), (8, rows)) - hits
+        for k in range(1, nz):
+            plane_copy(k).start()
+
+    first_piece()
     part_group(0)
+    part_group(1)
+    plane_loss()
+    core_sum(0)
+    part_group(2)
+    core_sum(1)
     head_piece(1, 0)
-    part_group(1)
-    for n in range(len(peers)):
-        loss_copy(n).start()
-    core_sum(0)
+    part_group(3)
+    core_sum(2)
     head_piece(2, 0)
-    for g in range(2, count):
+    relay(2, 0, 0)
+    for g in range(4, count):
         part_group(g)
         core_sum(g - 1)
-        if g == 3:
-            relay(0)
     core_sum(count - 1)
     head_piece(3, 0)
-
-    loss_all[me] = loss_one[...]
-    for n in range(len(peers)):
-        bb, vv, i = peer(n)
-        copy(loss_one, loss_all.at[i], ls.at[n], lr.at[i], bb, vv).wait_recv()
-    losses = loss_all[0]
-    for i in range(1, group):
-        losses = losses + loss_all[i]
-    loss_two[...] = losses
-
-    def plane_copy(k):
-        return copy(loss_two, loss_zs.at[z], ms.at[k - 1], mr.at[z], z_peer(k), v)
-
-    for k in range(1, nz):
-        plane_copy(k).start()
-
-    x_sum(0)
-    for n in range(steps):
-        delta_copy(n).wait_recv()
-    for k in range(nz):
-        head_piece(k, 1)
-        if k == 1:
-            x_sum(1)
-    x_sum(2)
-    relay(1)
-    for g in range(3, count):
-        x_sum(g)
-        y_sum(g - 3)
+    one_sum(0)
+
+    whole_delta = copy(delta.at[0], delta.at[1], es.at[0], er.at[0], over_y, v)
+    whole_delta.wait_recv()
+    head_piece(0, 1)
+    head_piece(1, 1)
+    one_sum(1)
+    head_piece(2, 1)
+    head_piece(3, 1)
+    one_sum(2)
+    relay(2, 1, 1)
+
+    copy(w_over, w_over, wys.at[0], wr.at[0, 0], over_y, v).wait_send()
+    for n in range(1, nz):
+        sent_rows = w_all.at[pl.ds(0, n * slab)]
+        for way, slabs_sent in ((0, z + 1), (1, nz - z)):
+            going = (slabs_sent == n) & (has_down if way else has_up)
+            pl.when(going)(lambda: copy(sent_rows, sent_rows, ws.at[way], wr.at[0, 0], b, over_x).wait_send())
+    seven = h_all.at[pl.ds(0, 7 * rows)]
+    copy(seven, seven, hs.at[0], hr.at[0], b, over_x).wait_send()
+    for got, sem in ((code_got, cs), (stat_all, ss), (loss_all, ls)):
+        copy(got.at[others], got.at[others], sem.at[0], sem.at[0], b, over_x).wait_send()
+    one_sum(3)
+    two_sum(0)
+    whole_delta.wait_send()
+    copy(core_in, core_in, ds.at[0], dr.at[0], b, over_core).wait_send()
+    one_sum(4)
+    two_sum(1)
+    two_sum(2)
+    relay(0, 1, 2)
+    for g in range(5, count):
+        one_sum(g)
+        two_sum(g - 2)
 
     def r_got(zz, r):
-        copy(r_in.at[zz, r], r_in.at[zz, r], rs.at[0, r], rr.at[zz, r], z_peer(1), v).wait_recv()
+        copy(r_in.at[zz, r], r_in.at[zz, r], rs.at[0], rr.at[zz, r], z_peer(1), v).wait_recv()
 
     def lanes(r):
         return pl.ds(pl.multiple_of(flip(y, r) * half, 128), half)
@@ -1009,8 +1076,17 @@
     sources = [near, jnp.where(low, 2, 1), far]
 
     def head_sum(r):
-        for k in range(2):
-            r_got(sources[k], r)
+        @pl.when(at_end)
+        def _():
+            r_got(sources[0], r)
+
+        @pl.when(inside)
+        def _():
+            for h in range(2):
+                mine = r_in.at[sources[0], r, pl.ds(h * piece, piece)]
+                copy(mine, mine, rs.at[0], nr.at[r, h], near_end * ny + y, v).wait_recv()
+
+        r_got(sources[1], r)
 
         def add(n):
             here = pl.ds(n, cstep)
@@ -1023,6 +1099,8 @@
 
         @pl.when(inside)
         def _():
+            if r:
+                return
             r_got(sources[2], r)
 
             def last(n):
@@ -1032,58 +1110,35 @@
             over_cols(last)
 
     head_sum(0)
-    y_sum(count - 3)
-    y_sum(count - 2)
     loss_zs[z] = loss_two[...]
-    for k in range(1, nz):
-        i = lax.rem(z + k, nz)
-        copy(loss_two, loss_zs.at[i], ms.at[k - 1], mr.at[i], z_peer(k), v).wait_recv()
+    along = loss_zs.at[pl.ds(0, nz - 1)]
+    copy(along, along, ms.at[0], mr.at[0], z_peer(1), v).wait_recv()
     losses = loss_zs[0]
     for i in range(1, nz):
         losses = losses + loss_zs[i]
     loss_out[...] = losses * (1.0 / (tokens * nz))
-    y_sum(count - 1)
+    copy(along, along, ms.at[0], mr.at[0], z_peer(1), v).wait_send()
+    two_sum(count - 2)
+    two_sum(count - 1)
     head_sum(1)
 
-    for h in range(2):
-        w_y(h).wait_send()
-        pl.when(has_up)(lambda: w_z(b, h, True).wait_send())
-        pl.when(has_down)(lambda: w_z(b, h, False).wait_send())
-        pl.when(has_up)(lambda: w_z(z * ny + 1 - y, h, True).wait_send())
-        pl.when(has_down)(lambda: w_z(z * ny + 1 - y, h, False).wait_send())
-
-    @pl.when(inside)
-    def _():
-        for j in range(1, nz):
-            for k in range(ny):
-                for h in range(2):
-                    w_pass(slabs[j] * ny + flip(y, k), h, slabs[j] < z).wait_send()
-
-    h_x().wait_send()
-    h_y().wait_send()
-    pl.when(core == 0)(lambda: h_xy().wait_send())
-    pl.when(core == 1)(lambda: h_yx().wait_send())
-    for kx, ky in blocks:
-        h_core(kx, ky).wait_send()
-    for n in range(len(peers)):
-        code_copy(n).wait_send()
-        stat_copy(n).wait_send()
-        loss_copy(n).wait_send()
-    for k in range(1, nz):
-        plane_copy(k).wait_send()
-    for n in range(steps):
-        delta_copy(n).wait_send()
-    for r in range(2):
-        pl.when(at_end)(lambda: far_copy(r).wait_send())
-        pl.when(inside)(lambda: r_copy(0, r).wait_send())
-        r_copy(1, r).wait_send()
-        r_copy(2, r).wait_send()
-    for g in range(count):
-        for kx, ky in blocks:
-            core_copy(g, kx, ky).wait_send()
-        for ky in range(2):
-            x_copy(g, ky).wait_send()
-        y_copy(g).wait_send()
+    for part_sent, sem in ((x_out, xs), (y_out, ys), (r_in.at[pl.ds(0, nz - 1)], rs)):
+        copy(part_sent, part_sent, sem.at[0], sem.at[0], b, over_x).wait_send()
+
+
+def finish_kernel(head_in, hid_in, loss_in, head_out, hid_out, loss_out, sem):
+    parts = sem.shape[1]
+    moves = []
+    for k, (src, dst) in enumerate(((hid_in, hid_out), (head_in, head_out))):
+        size = src.shape[0] // parts
+        for n in range(parts):
+            here = pl.ds(n * size, size)
+            moves.append(pltpu.make_async_copy(src.at[here], dst.at[here], sem.at[k, n]))
+    for one in moves:
+        one.start()
+    loss_out[0, 0] = loss_in[0, 0]
+    for one in moves:
+        one.wait()
 
 
 def plane_local(hidden, head_weight, targets, valid_mask):
@@ -1104,16 +1159,16 @@
         vm((1, rows), jnp.int32), vm((1, rows), jnp.int32), line, vm((group, 8, rows), f32), vm((tokens, 128), f32),
         vm((tokens, half), f32), vm((tokens, half), f32), vm((2, tokens, half), bf16),
         line, vm((group, 8, rows), f32), line, line, vm((group, 8, rows), f32), vm((nz, 8, rows), f32),
-        vm((2, win, half), f32), vm((2, win, half), f32), vm((3, 2, win, half), bf16),
-        vm((2, cols, half), bf16), vm((nz, 2, cols, half), bf16),
+        vm((2, win, half), f32), vm((3, win, half), f32), vm((3, 2, win, half), bf16),
+        vm((3, cols, half), bf16), vm((nz, 2, cols, half), bf16),
         vm((tokens, width), f32), vm((2, 2, rows, width), f32),
         vm((2, rows, width), bf16), vm((2, rows, width), bf16), vm((rows, width), bf16), vm((rows, width), bf16),
     ]
     sems = [
-        dma((5,)), dma((2,)), dma((1,)), dma((2, 2)), dma((group,)), dma((8, 2)), dma((8, 2)), dma((8, 2)), dma((2,)),
-        dma((7,)), dma((group,)), dma((7,)), dma((group,)), dma((7,)), dma((group,)), dma((3,)), dma((nz,)),
-        dma((4,)), dma((4,)), dma((3, 2)), dma((nz, 2)), dma((2,)), dma((2,)),
-        dma((count, 2, 2)), dma((count, 2, 2)), dma((count, 2)), dma((count, 2)), dma((count,)), dma((count,)),
+        dma((5,)), dma((1,)), dma((group,)), dma((2,)), dma((8, 2)), dma((1,)),
+        dma((1,)), dma((1,)), dma((1,)), dma((1,)), dma((1,)), dma((1,)), dma((1,)), dma((1,)),
+        dma((1,)), dma((1,)), dma((1,)), dma((nz, 2)), dma((2, 2)), dma((4,)),
+        dma((1,)), dma((count,)), dma((1,)), dma((count, 2)), dma((1,)), dma((count,)),
     ]
     whole = pl.BlockSpec(memory_space=vm)
     head_t, hidden_grad, loss = pl.pallas_call(
@@ -1129,6 +1184,19 @@
         compiler_params=pltpu.CompilerParams(
             collective_id=1, has_side_effects=True, vmem_limit_bytes=58 * 1024 * 1024),
     )(hidden, jnp.transpose(head_weight), targets[None, :], valid_mask[None, :])
+    anywhere = pl.BlockSpec(memory_space=pl.ANY)
+    head_t, hidden_grad, loss = pl.pallas_call(
+        finish_kernel,
+        out_shape=(
+            jax.ShapeDtypeStruct((cols, entries), f32),
+            jax.ShapeDtypeStruct((rows, width), f32),
+            jax.ShapeDtypeStruct((1, 1), f32),
+        ),
+        in_specs=[whole] * 3,
+        out_specs=(anywhere, anywhere, pl.BlockSpec(memory_space=pltpu.SMEM)),
+        scratch_shapes=[dma((2, 4))],
+        compiler_params=pltpu.CompilerParams(vmem_limit_bytes=1024 * 1024),
+    )(head_t, hidden_grad, loss)
     return jnp.transpose(head_t), hidden_grad, loss[0, 0]
 
 
@@ -1136,7 +1204,7 @@
     rows, width = hidden.shape
     entries, cols = head_weight.shape
     fits = nb == 8 and nv == 4 and rows == 128 and width % 256 == 0 and width >= 2048
-    return fits and entries % 256 == 0 and cols % 32 == 0 and (2 * cols) % 128 == 0
+    return fits and entries % 256 == 0 and entries >= 512 and cols % 32 == 0 and (2 * cols) % 128 == 0
 
 
 def device(nb, nv, *arrays):

time: 111 us -> 107 us (0.964)
  local copies, waits for them, and re-layouts: 2.82 us -> 0 us
  Pallas kernels: 108 us -> 106 us
    pallas_call x1, Pallas kernels: 108 us -> 103 us  [plane_local(): pl.pallas_call(plane_kernel, out_shape=(vm((cols, entries), f32), vm((row...]
    unnamed x2 -> x0, local copies, waits for them, and re-layouts: 2.31 us -> none
    pallas_call x0 -> x1, Pallas kernels: none -> 2.26 us  [plane_local(): pl.pallas_call(finish_kernel, out_shape=(jax.ShapeDtypeStruct((cols, entr...]
where the time goes in v3:
time: 107 us; the launch traced here: 106 us
  Pallas kernels  106 us (99%)
    pallas_call x1, Pallas kernels, plane_local(): pl.pallas_call(plane_kernel, out_shape=(vm((cols, entries), f32), vm((row...  103 us
    pallas_call x1, Pallas kernels, plane_local(): pl.pallas_call(finish_kernel, out_shape=(jax.ShapeDtypeStruct((cols, entr...  2.26 us

profile of v3, /device:TPU:0, one launch (start us, length us, event | category | flops | bytes accessed | tf_op | source)
XLA Modules:
  0.0 106.4 jit_solution(5359091554936714324)
XLA Ops:
  0.6 103.5 %shard_map.67 = (f32[448,768]{1,0:T(8,128)S(1)}, f32[128,3584]{1,0:T(8,128)S(1)}, f32[8,128]{1,0:T(8,128)S(1)}) custom-call(bf16[128,3584]{1,0:T(8,128)(2,1)} %h_in.1, bf16[448,768]{1,0:T(8,128)(2,1)} %bitcast.5, s32[1,128]{1,0:T(1,128)} %bitcast.6, s32[1,128]{1,0:T(1,128)} %bitcast.7), custom_call_target="tpu_custom_call" | custom-call | tf_op jit(solution)/shard_map/pallas_call | solution.py:1174
  104.1 2.3 %shard_map.68 = (f32[448,768]{1,0:T(8,128)}, f32[128,3584]{1,0:T(8,128)}, f32[1,1]{1,0:T(1,128)}) custom-call(f32[448,768]{1,0:T(8,128)S(1)} %get-tuple-element.9.head_in, f32[128,3584]{1,0:T(8,128)S(1)} %get-tuple-element.10.hid_in, f32[8,128]{1,0:T(8,128)S(1)} %get-tuple-element.11.loss_in), custom_call_target="tpu_custom_call" | custom-call | tf_op jit(solution)/shard_map/pallas_call | solution.py:1188

commit v4 on v3

--- a/solution.py
+++ b/solution.py
@@ -541,7 +541,7 @@
                  logits, expo, delta, stat_own, stat_all, loss_one, loss_two, loss_all, loss_zs,
                  grad_own, held, grad_send, far_in, r_in, part, core_in, x_out, x_in, y_out, y_in, *sems):
     (own_sem, hs, hr, ws, wr, wys, cs, cr, ss, sr, ls, lr, ms, mr,
-     es, er, rs, rr, nr, fr, ds, dr, xs, xr, ys, yr) = sems
+     es, rs, rr, nr, fr, ds, xs, xr, ys) = sems
     nz, ny, nv = 4, 2, 4
     nb = nz * ny
     rows, width = h_in.shape
@@ -582,12 +582,17 @@
     def z_peer(k):
         return lax.rem(z + k, nz) * ny + y
 
+    has_up, has_down = z + 1 < nz, z >= 1
     barrier = pltpu.get_barrier_semaphore()
-    for k in range(1, nz):
-        pl.semaphore_signal(barrier, inc=1, device_id={"batch": z_peer(k), "vocab": v}, device_id_type=MESH)
-    for n in range(len(peers)):
-        bb, vv, _ = peer(n)
+
+    def greet(bb, vv):
         pl.semaphore_signal(barrier, inc=1, device_id={"batch": bb, "vocab": vv}, device_id_type=MESH)
+
+    pl.when(has_up)(lambda: greet(b + ny, v))
+    pl.when(has_down)(lambda: greet(b - ny, v))
+    greet(over_y, v)
+    greet(b, over_x)
+    greet(b, over_core)
     first = pl.ds(pl.multiple_of(y * half, 128), half)
     second = pl.ds(pl.multiple_of((1 - y) * half, 128), half)
     local = [
@@ -603,7 +608,7 @@
         one.wait()
     code = jnp.where(mask_own[...] != 0, ids_own[...], -1).astype(f32)
     code_own[...] = jnp.broadcast_to(code, code_own.shape)
-    pl.semaphore_wait(barrier, nz - 1 + len(peers))
+    pl.semaphore_wait(barrier, jnp.where(inside, 5, 4))
 
     def w_ref(i, h):
         return w_all.at[pl.ds(pl.multiple_of(i * cols + h * piece, 16), piece)]
@@ -621,7 +626,6 @@
     def w_got(i, h):
         copy(w_ref(i, h), w_ref(i, h), wys.at[0], wr.at[i, h], over_y, v).wait_recv()
 
-    has_up, has_down = z + 1 < nz, z >= 1
     near = z + 1 - 2 * lax.rem(z, 2)
     slabs = [z, near, jnp.where(low, 2, 1), jnp.where(low, 3, 0)]
 
@@ -659,9 +663,14 @@
         pl.when(has_down)(lambda: w_z(b, h, False).start())
     h_x().start()
     h_y().start()
-    for n in range(len(peers)):
-        code_copy(n).start()
     h_core(0, 0).start()
+
+    def send_codes(count):
+        for n in range(len(peers)):
+            if sum(peers[n]) == count:
+                code_copy(n).start()
+
+    send_codes(1)
     for h in range(2):
         i = z * ny + 1 - y
         w_got(i, h)
@@ -691,6 +700,7 @@
     h_got(0, 1, core)
     pl.when(core == 1)(lambda: h_yx().start())
     h_core(0, 1).start()
+    send_codes(2)
 
     @pl.when(at_end)
     def _():
@@ -700,14 +710,9 @@
     def _():
         w_slab(slabs[3], True)
 
-    code_got[me] = code_own[...]
-    others = pl.ds(0, group - 1)
-    copy(code_got.at[others], code_got.at[others], cs.at[0], cr.at[0], b, over_x).wait_recv()
-    for i in range(group):
-        code_all[i * rows:(i + 1) * rows, :] = jnp.transpose(jnp.concatenate([code_got[i]] * (rows // 8), axis=0))
-
     h_got(1, 1, core)
     h_core(1, 1).start()
+    send_codes(3)
     for kx in range(2):
         for ky in range(2):
             h_got(kx, ky, 1 - core)
@@ -728,6 +733,12 @@
                 logits[span, :] += scores(n, slabs[j])
             else:
                 logits[span, :] = scores(n, slabs[j])
+
+    code_got[me] = code_own[...]
+    others = pl.ds(0, group - 1)
+    copy(code_got.at[others], code_got.at[others], cs.at[0], cr.at[0], b, over_x).wait_recv()
+    for i in range(group):
+        code_all[i * rows:(i + 1) * rows, :] = jnp.transpose(jnp.concatenate([code_got[i]] * (rows // 8), axis=0))
 
     early = lo
     pl.when(at_end)(lambda: w_slab(slabs[3], False, (0,)))
@@ -788,7 +799,7 @@
 
     def delta_copy(n):
         span = pl.ds(n * step, step)
-        return copy(delta.at[0, span], delta.at[1, span], es.at[0], er.at[0], over_y, v)
+        return copy(delta.at[0, span], delta.at[1, span], es.at[0], cr.at[0], over_y, v)
 
     for n in range(steps):
         for k in range(2):
@@ -916,7 +927,7 @@
 
     def core_copy(g, one, two):
         return copy(part.at[hrow(block(g, one, two, 1 - core)), span_of(g)], core_in.at[one, two, :, span_of(g)],
-                    ds.at[0], dr.at[g], b, over_core)
+                    ds.at[0], wr.at[g, 0], b, over_core)
 
     def over_one(g):
         return (over_y, v) if g in y_first else (b, over_x)
@@ -925,11 +936,11 @@
         return (b, over_x) if g in y_first else (over_y, v)
 
     def one_copy(g, two):
-        return copy(x_out.at[two, :, span_of(g)], x_in.at[two, :, span_of(g)], xs.at[0], xr.at[g, two],
+        return copy(x_out.at[two, :, span_of(g)], x_in.at[two, :, span_of(g)], xs.at[0], (hr if two else xr).at[g],
                     *over_one(g))
 
     def two_copy(g):
-        return copy(y_out.at[:, span_of(g)], y_in.at[:, span_of(g)], ys.at[0], yr.at[g], *over_two(g))
+        return copy(y_out.at[:, span_of(g)], y_in.at[:, span_of(g)], ys.at[0], wr.at[g, 1], *over_two(g))
 
     def part_group(g):
         first, n = groups[g]
@@ -956,7 +967,7 @@
     def core_sum(g):
         span = span_of(g)
         landed = core_in.at[:, :, :, span]
-        copy(landed, landed, ds.at[0], dr.at[g], b, over_core).wait_recv()
+        copy(landed, landed, ds.at[0], wr.at[g, 0], b, over_core).wait_recv()
         for one, two in blocks:
             start = block(g, one, two, core) * rows
 
@@ -1035,7 +1046,7 @@
     head_piece(3, 0)
     one_sum(0)
 
-    whole_delta = copy(delta.at[0], delta.at[1], es.at[0], er.at[0], over_y, v)
+    whole_delta = copy(delta.at[0], delta.at[1], es.at[0], cr.at[0], over_y, v)
     whole_delta.wait_recv()
     head_piece(0, 1)
     head_piece(1, 1)
@@ -1058,7 +1069,7 @@
     one_sum(3)
     two_sum(0)
     whole_delta.wait_send()
-    copy(core_in, core_in, ds.at[0], dr.at[0], b, over_core).wait_send()
+    copy(core_in, core_in, ds.at[0], wr.at[0, 0], b, over_core).wait_send()
     one_sum(4)
     two_sum(1)
     two_sum(2)
@@ -1167,8 +1178,8 @@
     sems = [
         dma((5,)), dma((1,)), dma((group,)), dma((2,)), dma((8, 2)), dma((1,)),
         dma((1,)), dma((1,)), dma((1,)), dma((1,)), dma((1,)), dma((1,)), dma((1,)), dma((1,)),
-        dma((1,)), dma((1,)), dma((1,)), dma((nz, 2)), dma((2, 2)), dma((4,)),
-        dma((1,)), dma((count,)), dma((1,)), dma((count, 2)), dma((1,)), dma((count,)),
+        dma((1,)), dma((1,)), dma((nz, 2)), dma((2, 2)), dma((4,)),
+        dma((1,)), dma((1,)), dma((count,)), dma((1,)),
     ]
     whole = pl.BlockSpec(memory_space=vm)
     head_t, hidden_grad, loss = pl.pallas_call(
@@ -1204,6 +1215,7 @@
     rows, width = hidden.shape
     entries, cols = head_weight.shape
     fits = nb == 8 and nv == 4 and rows == 128 and width % 256 == 0 and width >= 2048
+    fits = fits and len(column_groups(width)) <= 8
     return fits and entries % 256 == 0 and entries >= 512 and cols % 32 == 0 and (2 * cols) % 128 == 0
 
 

time: 107 us -> 105 us (0.981)
  Pallas kernels: 106 us -> 104 us
    pallas_call x1, Pallas kernels: 103 us -> 102 us  [plane_local(): pl.pallas_call(plane_kernel, out_shape=(vm((cols, entries), f32), vm((row...]
where the time goes in v4:
time: 105 us; the launch traced here: 104 us
  Pallas kernels  104 us (99%)
    pallas_call x1, Pallas kernels, plane_local(): pl.pallas_call(plane_kernel, out_shape=(vm((cols, entries), f32), vm((row...  102 us
    pallas_call x1, Pallas kernels, plane_local(): pl.pallas_call(finish_kernel, out_shape=(jax.ShapeDtypeStruct((cols, entr...  2.26 us

profile of v4, /device:TPU:0, one launch (start us, length us, event | category | flops | bytes accessed | tf_op | source)
XLA Modules:
  0.0 104.5 jit_solution(5760197858444929698)
XLA Ops:
  0.6 101.6 %shard_map.67 = (f32[448,768]{1,0:T(8,128)S(1)}, f32[128,3584]{1,0:T(8,128)S(1)}, f32[8,128]{1,0:T(8,128)S(1)}) custom-call(bf16[128,3584]{1,0:T(8,128)(2,1)} %h_in.1, bf16[448,768]{1,0:T(8,128)(2,1)} %bitcast.5, s32[1,128]{1,0:T(1,128)} %bitcast.6, s32[1,128]{1,0:T(1,128)} %bitcast.7), custom_call_target="tpu_custom_call" | custom-call | tf_op jit(solution)/shard_map/pallas_call | solution.py:1185
  102.2 2.3 %shard_map.68 = (f32[448,768]{1,0:T(8,128)}, f32[128,3584]{1,0:T(8,128)}, f32[1,1]{1,0:T(1,128)}) custom-call(f32[448,768]{1,0:T(8,128)S(1)} %get-tuple-element.9.head_in, f32[128,3584]{1,0:T(8,128)S(1)} %get-tuple-element.10.hid_in, f32[8,128]{1,0:T(8,128)S(1)} %get-tuple-element.11.loss_in), custom_call_target="tpu_custom_call" | custom-call | tf_op jit(solution)/shard_map/pallas_call | solution.py:1199

commit v5 on v4

--- a/solution.py
+++ b/solution.py
@@ -526,12 +526,12 @@
 
 
 def column_groups(width):
-    units = width // 256
-    sizes, left = [1, 2], units - 5
+    left = width // 256 - 11
+    sizes = [1, 2, 3, 2]
     while left > 0:
         sizes.append(min(3, left))
         left -= sizes[-1]
-    sizes += [1, 1]
+    sizes += [2, 1]
     starts = [sum(sizes[:n]) for n in range(len(sizes))]
     return [(s, n) for s, n in zip(starts, sizes)]
 
@@ -539,9 +539,9 @@
 def plane_kernel(h_in, w_in, ids_in, mask_in, head_out, hid_out, loss_out, h_all, w_all, w_over, ids_own, mask_own,
                  code_own, code_got, code_all,
                  logits, expo, delta, stat_own, stat_all, loss_one, loss_two, loss_all, loss_zs,
-                 grad_own, held, grad_send, far_in, r_in, part, core_in, x_out, x_in, y_out, y_in, *sems):
+                 grad_own, held, grad_send, far_in, r_in, h_end, d_end, part, core_in, x_out, x_in, y_out, y_in, *sems):
     (own_sem, hs, hr, ws, wr, wys, cs, cr, ss, sr, ls, lr, ms, mr,
-     es, rs, rr, nr, fr, ds, xs, xr, ys) = sems
+     es, er, rs, rr, fr, zs, zr, us, ur, ds, xs, xr, ys) = sems
     nz, ny, nv = 4, 2, 4
     nb = nz * ny
     rows, width = h_in.shape
@@ -571,6 +571,9 @@
     def hrow(i):
         return pl.ds(pl.multiple_of(i * rows, 16), rows)
 
+    far = jnp.where(low, nz - 1, 0)
+    across = jnp.where(low, 2, 1)
+    near_end = jnp.where(low, 1, 2)
     over_x, over_y, over_core = (1 - x) * 2 + core, z * ny + 1 - y, x * 2 + 1 - core
     peers = [(ky, kx, kc) for ky in range(2) for kx in range(2) for kc in range(2) if ky or kx or kc]
 
@@ -652,6 +655,32 @@
         i = flip(y, ky) * nv + flip(x, kx) * 2 + cc
         h_send(i, b, over_core).wait_recv()
 
+    def window(zz):
+        return pl.ds(pl.multiple_of(zz * slab + y * lo, 128), win)
+
+    def mine_of(kx, ky):
+        return flip(y, ky) * nv + flip(x, kx) * 2 + core
+
+    def h_out(kx, ky, j):
+        i = mine_of(kx, ky)
+        return copy(h_all.at[hrow(i), window((far, across, near_end)[j])], h_end.at[hrow(i), pl.ds(j * win, win)],
+                    us.at[0], ur.at[i], near_end * ny + y, v)
+
+    def send_out(kx, ky):
+        @pl.when(at_end)
+        def _():
+            for j in range(3):
+                h_out(kx, ky, j).start()
+
+    def end_copy(i):
+        return copy(h_end.at[hrow(i)], h_end.at[hrow(i)], us.at[0], ur.at[i], b, over_core)
+
+    def share_end(kx, ky):
+        @pl.when(inside)
+        def _():
+            end_copy(mine_of(kx, ky)).wait_recv()
+            end_copy(mine_of(kx, ky)).start()
+
     def code_copy(n):
         bb, vv, _ = peer(n)
         return copy(code_own, code_got.at[me], cs.at[0], cr.at[0], bb, vv)
@@ -676,6 +705,7 @@
         w_got(i, h)
         pl.when(has_up)(lambda: w_z(i, h, True).start())
         pl.when(has_down)(lambda: w_z(i, h, False).start())
+    send_out(0, 0)
 
     def w_slab(zz, onward, which=(0, 1)):
         for k in which:
@@ -697,9 +727,11 @@
     h_got(1, 0, core)
     pl.when(core == 0)(lambda: h_xy().start())
     h_core(1, 0).start()
+    send_out(1, 0)
     h_got(0, 1, core)
     pl.when(core == 1)(lambda: h_yx().start())
     h_core(0, 1).start()
+    send_out(0, 1)
     send_codes(2)
 
     @pl.when(at_end)
@@ -712,6 +744,7 @@
 
     h_got(1, 1, core)
     h_core(1, 1).start()
+    send_out(1, 1)
     send_codes(3)
     for kx in range(2):
         for ky in range(2):
@@ -790,6 +823,8 @@
         code_rows = jnp.where(lines == i, code_got[i], code_rows)
     weight = (code_rows >= 0).astype(f32)
 
+    share_end(0, 0)
+    share_end(1, 0)
     stat_all[me] = sums
     copy(stat_all.at[others], stat_all.at[others], ss.at[0], sr.at[0], b, over_x).wait_recv()
     partition = stat_all[0]
@@ -797,9 +832,11 @@
         partition = partition + stat_all[i]
     scale = weight / partition
 
-    def delta_copy(n):
-        span = pl.ds(n * step, step)
-        return copy(delta.at[0, span], delta.at[1, span], es.at[0], cr.at[0], over_y, v)
+    lane_parts = [pl.ds(0, half - 128), pl.ds(half - 128, 128)]
+
+    def delta_copy(p):
+        here = lane_parts[p]
+        return copy(delta.at[0, :, here], delta.at[1, :, here], es.at[0], (cr, er)[p].at[0], over_y, v)
 
     for n in range(steps):
         for k in range(2):
@@ -808,80 +845,103 @@
             by_row = jnp.transpose(jnp.broadcast_to(scale[i:i + 1, :], (rows, rows)))
             factor = jnp.concatenate([by_row] * (half // rows), axis=1)
             delta[0, span, :] = (expo[span, :] * factor - logits[span, :]).astype(bf16)
-        delta_copy(n).start()
-
-    near_end = jnp.where(low, 1, 2)
-    far = jnp.where(low, nz - 1, 0)
-    across = jnp.where(low, 2, 1)
+    for p in range(2):
+        delta_copy(p).start()
+
+    chunks = range(half // 128)
+
+    def chunk_of_delta(n):
+        here = pl.ds(n * 128, 128)
+        return copy(delta.at[0, :, here], d_end.at[:, here], zs.at[0], zr.at[n], near_end * ny + y, v)
+
+    for n in chunks:
+        pl.when(at_end)(lambda: chunk_of_delta(n).start())
+
     targets = [jnp.where(at_end, far, across), jnp.where(at_end, across, near), jnp.where(at_end, near_end, far), z]
     top = y * shift
 
-    def grad_share(zz, r, first, wide):
-        here = pl.ds(pl.multiple_of(zz * slab + y * lo, 128), win)
-        return lax.dot_general(h_all[:, here], delta[r, :, first:first + wide], (((0,), (0,)), ((), ())), preferred_element_type=f32)
+    def over_tokens(left, right):
+        return lax.dot_general(left, right, (((0,), (0,)), ((), ())), preferred_element_type=f32)
+
+    def grad_share(zz, r):
+        return over_tokens(h_all[:, window(zz)], delta[r])
 
     def sent(k, r):
         return grad_send.at[k, r, pl.ds(pl.multiple_of(top, 16), cols)]
 
     def r_copy(k, r):
-        return copy(sent(k, r), r_in.at[z, r], rs.at[0], rr.at[z, r], targets[k] * ny + y, v)
-
-    def far_copy(r):
-        return copy(sent(0, r), far_in.at[r], rs.at[0], fr.at[r], near_end * ny + y, v)
-
-    bounds = [(0, 128), (128, half - 128)]
-
-    def far_part(n):
-        here = pl.ds(*bounds[n])
-        return copy(grad_send.at[0, 0, pl.ds(pl.multiple_of(top, 16), cols), here], far_in.at[0, :, here],
-                    rs.at[0], fr.at[(0, 2)[n]], near_end * ny + y, v)
-
-    def cross_copy():
-        return copy(sent(1, 1), far_in.at[2], rs.at[0], fr.at[3], near_end * ny + y, v)
-
-    def near_copy(r, h):
-        src = grad_send.at[2, r, pl.ds(pl.multiple_of(top + h * piece, 16), piece)]
-        return copy(src, r_in.at[z, r, pl.ds(h * piece, piece)], rs.at[0], nr.at[r, h], near_end * ny + y, v)
-
-    def first_piece():
-        for n in range(2):
-            first, wide = bounds[n]
-            grad_send[0, 0, :, first:first + wide] = grad_share(targets[0], 0, first, wide).astype(bf16)
-            pl.when(at_end)(lambda: far_part(n).start())
-        pl.when(inside)(lambda: r_copy(0, 0).start())
-
-    def head_piece(k, r):
-        share = grad_share(targets[k], r, 0, half)
-        if k == nz - 1:
-            grad_own[r] = share
-        elif k == 2:
+        return copy(sent(k, r), r_in.at[z * 2 + r], rs.at[0], rr.at[z, r], targets[k] * ny + y, v)
+
+    def relay_copy(n, p):
+        src = grad_send.at[n, 1, pl.ds(pl.multiple_of(top, 16), cols), lane_parts[p]]
+        return copy(src, far_in.at[n, :, lane_parts[p]], rs.at[0], fr.at[n, p], near_end * ny + y, v)
+
+    def part_copy(k, p):
+        src = grad_send.at[k, 1, pl.ds(pl.multiple_of(top, 16), cols), lane_parts[p]]
+        return copy(src, r_in.at[z * 2 + 1, :, lane_parts[p]], rs.at[0], rr.at[z, 1], targets[k] * ny + y, v)
+
+    def chunk_copy(k, n):
+        here = pl.ds(n * 128, 128)
+        src = grad_send.at[k, 0, pl.ds(pl.multiple_of(top, 16), cols), here]
+        return copy(src, r_in.at[z * 2, :, here], rs.at[0], rr.at[z, 0], targets[k] * ny + y, v)
+
+    def to_end():
+        @pl.when(inside)
+        def _():
+            grad_send[1, 0] = grad_share(near, 0).astype(bf16)
+            r_copy(1, 0).start()
+
+    def keep():
+        @pl.when(inside)
+        def _():
+            held[0] = grad_share(across, 0)
+            held[1] = grad_share(far, 0)
+
+    def chunk(n):
+        first = n * 128
+
+        @pl.when(inside)
+        def _():
+            if n == 0:
+                for kx in range(2):
+                    for ky in range(2):
+                        end_copy(flip(y, ky) * nv + flip(x, kx) * 2 + 1 - core).wait_recv()
+            chunk_of_delta(n).wait_recv()
+            right = d_end[:, first:first + 128]
+            for k, slot, j in ((0, 0, 1), (2, 1, 0)):
+                share = held[slot, :, first:first + 128] + over_tokens(h_end[:, j * win:(j + 1) * win], right)
+                grad_send[k, 0, :, first:first + 128] = share.astype(bf16)
+                chunk_copy(k, n).start()
+            grad_own[0, :, first:first + 128] += over_tokens(h_end[:, 2 * win:3 * win], right)
+
+    def head_part(k, p):
+        here = lane_parts[p]
+        share = over_tokens(h_all[:, window(targets[k])], delta[1, :, here])
+        if k:
+            grad_send[k, 1, :, here] = share.astype(bf16)
+            pl.when(at_end)(lambda: relay_copy(1, p).start())
+            pl.when(inside)(lambda: part_copy(k, p).start())
+        else:
             @pl.when(at_end)
             def _():
-                grad_send[k, r] = share.astype(bf16)
-                near_copy(r, 0).start()
-                if r:
-                    near_copy(0, 1).start()
-                    near_copy(1, 1).start()
+                grad_send[k, 1, :, here] = share.astype(bf16)
+                relay_copy(0, p).start()
 
             @pl.when(inside)
             def _():
-                held[r] = share
-        elif k == 0:
-            @pl.when(at_end)
-            def _():
-                grad_send[k, r] = share.astype(bf16)
-                far_copy(r).start()
-
-            @pl.when(inside)
-            def _():
-                held[2] = share
-        else:
-            grad_send[k, r] = share.astype(bf16)
-            if r:
-                pl.when(at_end)(lambda: cross_copy().start())
-                pl.when(inside)(lambda: r_copy(k, r).start())
-            else:
-                r_copy(k, r).start()
+                held[0, :, here] = share
+
+    def head_rest():
+        share = grad_share(targets[2], 1)
+
+        @pl.when(at_end)
+        def _():
+            grad_send[2, 1] = share.astype(bf16)
+            r_copy(2, 1).start()
+
+        @pl.when(inside)
+        def _():
+            held[1] = share
 
     cstep = chunk_of(cols, 64)
 
@@ -892,24 +952,21 @@
 
         lax.fori_loop(0, cols // cstep, one, 0)
 
-    def relay(k, r, slot):
+    def relay(k, n, p):
+        lane = lane_parts[p]
+
         @pl.when(inside)
         def _():
-            if r == 0:
-                for n in range(2):
-                    far_part(n).wait_recv()
-            elif k:
-                far_copy(r).wait_recv()
-            else:
-                cross_copy().wait_recv()
-
-            def add(n):
-                here = pl.ds(pl.multiple_of(top + n, 16), cstep)
-                there = pl.ds(n, cstep)
-                grad_send[k, r, here, :] = (held[slot, here, :] + far_in[slot, there, :].astype(f32)).astype(bf16)
+            relay_copy(n, p).wait_recv()
+
+            def add(m):
+                here = pl.ds(pl.multiple_of(top + m, 16), cstep)
+                there = pl.ds(m, cstep)
+                grad_send[k, 1, here, lane] = (
+                    held[k // 2, here, lane] + far_in[n, there, lane].astype(f32)).astype(bf16)
 
             over_cols(add)
-            r_copy(k, r).start()
+            part_copy(k, p).start()
 
     groups = column_groups(width)
     blocks = [(1, 1), (1, 0), (0, 1), (0, 0)]
@@ -1027,34 +1084,42 @@
         for k in range(1, nz):
             plane_copy(k).start()
 
-    first_piece()
     part_group(0)
     part_group(1)
+    to_end()
     plane_loss()
     core_sum(0)
     part_group(2)
     core_sum(1)
-    head_piece(1, 0)
+    share_end(0, 1)
+    keep()
     part_group(3)
     core_sum(2)
-    head_piece(2, 0)
-    relay(2, 0, 0)
-    for g in range(4, count):
+    share_end(1, 1)
+    grad_own[0] = grad_share(z, 0)
+    part_group(4)
+    core_sum(3)
+    chunk(0)
+    for g in range(5, count):
         part_group(g)
         core_sum(g - 1)
     core_sum(count - 1)
-    head_piece(3, 0)
+    for n in chunks[1:-1]:
+        chunk(n)
     one_sum(0)
 
-    whole_delta = copy(delta.at[0], delta.at[1], es.at[0], cr.at[0], over_y, v)
-    whole_delta.wait_recv()
-    head_piece(0, 1)
-    head_piece(1, 1)
+    delta_copy(0).wait_recv()
+    head_part(0, 0)
+    head_part(1, 0)
+    chunk(len(chunks) - 1)
+    delta_copy(1).wait_recv()
+    head_part(0, 1)
+    head_part(1, 1)
     one_sum(1)
-    head_piece(2, 1)
-    head_piece(3, 1)
+    head_rest()
+    grad_own[1] = grad_share(z, 1)
     one_sum(2)
-    relay(2, 1, 1)
+    relay(2, 0, 0)
 
     copy(w_over, w_over, wys.at[0], wr.at[0, 0], over_y, v).wait_send()
     for n in range(1, nz):
@@ -1068,57 +1133,49 @@
         copy(got.at[others], got.at[others], sem.at[0], sem.at[0], b, over_x).wait_send()
     one_sum(3)
     two_sum(0)
-    whole_delta.wait_send()
+    copy(delta.at[0], delta.at[1], es.at[0], cr.at[0], over_y, v).wait_send()
+    relay(0, 1, 0)
     copy(core_in, core_in, ds.at[0], wr.at[0, 0], b, over_core).wait_send()
     one_sum(4)
     two_sum(1)
-    two_sum(2)
-    relay(0, 1, 2)
+    relay(2, 0, 1)
+    relay(0, 1, 1)
     for g in range(5, count):
         one_sum(g)
-        two_sum(g - 2)
+    two_sum(2)
+    for g in range(4, count - 1):
+        two_sum(g)
 
     def r_got(zz, r):
-        copy(r_in.at[zz, r], r_in.at[zz, r], rs.at[0], rr.at[zz, r], z_peer(1), v).wait_recv()
+        whole = r_in.at[zz * 2 + r]
+        copy(whole, whole, rs.at[0], rr.at[zz, r], z_peer(1), v).wait_recv()
 
     def lanes(r):
         return pl.ds(pl.multiple_of(flip(y, r) * half, 128), half)
 
-    sources = [near, jnp.where(low, 2, 1), far]
-
     def head_sum(r):
-        @pl.when(at_end)
-        def _():
-            r_got(sources[0], r)
-
-        @pl.when(inside)
-        def _():
-            for h in range(2):
-                mine = r_in.at[sources[0], r, pl.ds(h * piece, piece)]
-                copy(mine, mine, rs.at[0], nr.at[r, h], near_end * ny + y, v).wait_recv()
-
-        r_got(sources[1], r)
+        r_got(across, r)
 
         def add(n):
             here = pl.ds(n, cstep)
             total = grad_own[r, pl.ds(pl.multiple_of(top + n, 16), cstep), :]
-            for k in range(2):
-                total = total + r_in[sources[k], r, here, :].astype(f32)
-            head_out[here, lanes(r)] = total
+            head_out[here, lanes(r)] = total + r_in[across * 2 + r, here, :].astype(f32)
 
         over_cols(add)
 
-        @pl.when(inside)
-        def _():
-            if r:
-                return
-            r_got(sources[2], r)
+        def by_near():
+            r_got(near, r)
 
             def last(n):
                 here = pl.ds(n, cstep)
-                head_out[here, lanes(r)] += r_in[sources[2], r, here, :].astype(f32)
+                head_out[here, lanes(r)] += r_in[near * 2 + r, here, :].astype(f32)
 
             over_cols(last)
+
+        if r:
+            by_near()
+        else:
+            pl.when(at_end)(by_near)
 
     head_sum(0)
     loss_zs[z] = loss_two[...]
@@ -1129,12 +1186,23 @@
         losses = losses + loss_zs[i]
     loss_out[...] = losses * (1.0 / (tokens * nz))
     copy(along, along, ms.at[0], mr.at[0], z_peer(1), v).wait_send()
-    two_sum(count - 2)
+    two_sum(3)
     two_sum(count - 1)
     head_sum(1)
 
-    for part_sent, sem in ((x_out, xs), (y_out, ys), (r_in.at[pl.ds(0, nz - 1)], rs)):
+    rows_out = h_end.at[pl.ds(0, tokens // 2)]
+    for part_sent, sem in ((x_out, xs), (y_out, ys), (rows_out, us)):
         copy(part_sent, part_sent, sem.at[0], sem.at[0], b, over_x).wait_send()
+
+    @pl.when(at_end)
+    def _():
+        for part_sent, sem in ((d_end, zs), (r_in.at[pl.ds(0, 3)], rs)):
+            copy(part_sent, part_sent, sem.at[0], sem.at[0], b, over_x).wait_send()
+
+    @pl.when(inside)
+    def _():
+        six = r_in.at[pl.ds(0, 6)]
+        copy(six, six, rs.at[0], rs.at[0], b, over_x).wait_send()
 
 
 def finish_kernel(head_in, hid_in, loss_in, head_out, hid_out, loss_out, sem):
@@ -1170,15 +1238,15 @@
         vm((1, rows), jnp.int32), vm((1, rows), jnp.int32), line, vm((group, 8, rows), f32), vm((tokens, 128), f32),
         vm((tokens, half), f32), vm((tokens, half), f32), vm((2, tokens, half), bf16),
         line, vm((group, 8, rows), f32), line, line, vm((group, 8, rows), f32), vm((nz, 8, rows), f32),
-        vm((2, win, half), f32), vm((3, win, half), f32), vm((3, 2, win, half), bf16),
-        vm((3, cols, half), bf16), vm((nz, 2, cols, half), bf16),
+        vm((2, win, half), f32), vm((2, win, half), f32), vm((3, 2, win, half), bf16),
+        vm((2, cols, half), bf16), vm((nz * 2, cols, half), bf16), vm((tokens, 3 * win), bf16), vm((tokens, half), bf16),
         vm((tokens, width), f32), vm((2, 2, rows, width), f32),
         vm((2, rows, width), bf16), vm((2, rows, width), bf16), vm((rows, width), bf16), vm((rows, width), bf16),
     ]
     sems = [
         dma((5,)), dma((1,)), dma((group,)), dma((2,)), dma((8, 2)), dma((1,)),
         dma((1,)), dma((1,)), dma((1,)), dma((1,)), dma((1,)), dma((1,)), dma((1,)), dma((1,)),
-        dma((1,)), dma((1,)), dma((nz, 2)), dma((2, 2)), dma((4,)),
+        dma((1,)), dma((1,)), dma((1,)), dma((nz, 2)), dma((2, 2)), dma((1,)), dma((half // 128,)), dma((1,)), dma((group,)),
         dma((1,)), dma((1,)), dma((count,)), dma((1,)),
     ]
     whole = pl.BlockSpec(memory_space=vm)
@@ -1214,7 +1282,7 @@
 def in_planes(nb, nv, hidden, head_weight, targets, valid_mask):
     rows, width = hidden.shape
     entries, cols = head_weight.shape
-    fits = nb == 8 and nv == 4 and rows == 128 and width % 256 == 0 and width >= 2048
+    fits = nb == 8 and nv == 4 and rows == 128 and width % 256 == 0 and width >= 3072
     fits = fits and len(column_groups(width)) <= 8
     return fits and entries % 256 == 0 and entries >= 512 and cols % 32 == 0 and (2 * cols) % 128 == 0
 

time: 105 us -> 101 us (0.962)
  Pallas kernels: 104 us -> 100 us
    pallas_call x1, Pallas kernels: 102 us -> 98 us  [plane_local(): pl.pallas_call(plane_kernel, out_shape=(vm((cols, entries), f32), vm((row...]
where the time goes in v5:
time: 101 us
  Pallas kernels  100 us (99%)
    pallas_call x1, Pallas kernels, plane_local(): pl.pallas_call(plane_kernel, out_shape=(vm((cols, entries), f32), vm((row...  98 us
    pallas_call x1, Pallas kernels, plane_local(): pl.pallas_call(finish_kernel, out_shape=(jax.ShapeDtypeStruct((cols, entr...  2.26 us

profile of v5, /device:TPU:0, one launch (start us, length us, event | category | flops | bytes accessed | tf_op | source)
XLA Modules:
  0.0 101.1 jit_solution(866956906776561767)
XLA Ops:
  0.6 98.0 %shard_map.67 = (f32[448,768]{1,0:T(8,128)S(1)}, f32[128,3584]{1,0:T(8,128)S(1)}, f32[8,128]{1,0:T(8,128)S(1)}) custom-call(bf16[128,3584]{1,0:T(8,128)(2,1)} %h_in.1, bf16[448,768]{1,0:T(8,128)(2,1)} %bitcast.5, s32[1,128]{1,0:T(1,128)} %bitcast.6, s32[1,128]{1,0:T(1,128)} %bitcast.7), custom_call_target="tpu_custom_call" | custom-call | tf_op jit(solution)/shard_map/pallas_call | solution.py:1253
  98.7 2.3 %shard_map.68 = (f32[448,768]{1,0:T(8,128)}, f32[128,3584]{1,0:T(8,128)}, f32[1,1]{1,0:T(1,128)}) custom-call(f32[448,768]{1,0:T(8,128)S(1)} %get-tuple-element.9.head_in, f32[128,3584]{1,0:T(8,128)S(1)} %get-tuple-element.10.hid_in, f32[8,128]{1,0:T(8,128)S(1)} %get-tuple-element.11.loss_in), custom_call_target="tpu_custom_call" | custom-call | tf_op jit(solution)/shard_map/pallas_call | solution.py:1267

commit v6 on v5

--- a/solution.py
+++ b/solution.py
@@ -607,10 +607,8 @@
     ]
     for one in local:
         one.start()
-    for one in local:
+    for one in local[:2]:
         one.wait()
-    code = jnp.where(mask_own[...] != 0, ids_own[...], -1).astype(f32)
-    code_own[...] = jnp.broadcast_to(code, code_own.shape)
     pl.semaphore_wait(barrier, jnp.where(inside, 5, 4))
 
     def w_ref(i, h):
@@ -690,6 +688,10 @@
     for h in range(2):
         pl.when(has_up)(lambda: w_z(b, h, True).start())
         pl.when(has_down)(lambda: w_z(b, h, False).start())
+    for one in local[2:]:
+        one.wait()
+    code = jnp.where(mask_own[...] != 0, ids_own[...], -1).astype(f32)
+    code_own[...] = jnp.broadcast_to(code, code_own.shape)
     h_x().start()
     h_y().start()
     h_core(0, 0).start()
@@ -1205,17 +1207,16 @@
         copy(six, six, rs.at[0], rs.at[0], b, over_x).wait_send()
 
 
-def finish_kernel(head_in, hid_in, loss_in, head_out, hid_out, loss_out, sem):
-    parts = sem.shape[1]
-    moves = []
-    for k, (src, dst) in enumerate(((hid_in, hid_out), (head_in, head_out))):
-        size = src.shape[0] // parts
-        for n in range(parts):
-            here = pl.ds(n * size, size)
-            moves.append(pltpu.make_async_copy(src.at[here], dst.at[here], sem.at[k, n]))
-    for one in moves:
+def finish_kernel(head_in, hid_in, loss_in, head_out, hid_out, loss_out, loss_one, sem):
+    moves = [
+        pltpu.make_async_copy(hid_in, hid_out, sem.at[0]),
+        pltpu.make_async_copy(head_in, head_out, sem.at[1]),
+        pltpu.make_async_copy(loss_one, loss_out, sem.at[2]),
+    ]
+    for one in moves[:2]:
         one.start()
-    loss_out[0, 0] = loss_in[0, 0]
+    loss_one[...] = loss_in[0:1, 0:1]
+    moves[2].start()
     for one in moves:
         one.wait()
 
@@ -1272,8 +1273,8 @@
             jax.ShapeDtypeStruct((1, 1), f32),
         ),
         in_specs=[whole] * 3,
-        out_specs=(anywhere, anywhere, pl.BlockSpec(memory_space=pltpu.SMEM)),
-        scratch_shapes=[dma((2, 4))],
+        out_specs=(anywhere,) * 3,
+        scratch_shapes=[vm((1, 1), f32), dma((3,))],
         compiler_params=pltpu.CompilerParams(vmem_limit_bytes=1024 * 1024),
     )(head_t, hidden_grad, loss)
     return jnp.transpose(head_t), hidden_grad, loss[0, 0]

time: 101 us -> 100 us (0.990)
  no operation moved by 1% of the time
where the time goes in v6:
time: 100 us
  Pallas kernels  99.4 us (99%)
    pallas_call x1, Pallas kernels, plane_local(): pl.pallas_call(plane_kernel, out_shape=(vm((cols, entries), f32), vm((row...  97.7 us

profile of v6, /device:TPU:0, one launch (start us, length us, event | category | flops | bytes accessed | tf_op | source)
XLA Modules:
  0.0 100.2 jit_solution(11909931416705489309)
XLA Ops:
  0.6 97.7 %shard_map.67 = (f32[448,768]{1,0:T(8,128)S(1)}, f32[128,3584]{1,0:T(8,128)S(1)}, f32[8,128]{1,0:T(8,128)S(1)}) custom-call(bf16[128,3584]{1,0:T(8,128)(2,1)} %h_in.1, bf16[448,768]{1,0:T(8,128)(2,1)} %bitcast.5, s32[1,128]{1,0:T(1,128)} %bitcast.6, s32[1,128]{1,0:T(1,128)} %bitcast.7), custom_call_target="tpu_custom_call" | custom-call | tf_op jit(solution)/shard_map/pallas_call | solution.py:1254
  98.3 1.7 %shard_map.68 = (f32[448,768]{1,0:T(8,128)}, f32[128,3584]{1,0:T(8,128)}, f32[1,1]{1,0:T(1,128)}) custom-call(f32[448,768]{1,0:T(8,128)S(1)} %get-tuple-element.9.head_in, f32[128,3584]{1,0:T(8,128)S(1)} %get-tuple-element.10.hid_in, f32[8,128]{1,0:T(8,128)S(1)} %get-tuple-element.11.loss_in), custom_call_target="tpu_custom_call" | custom-call | tf_op jit(solution)/shard_map/pallas_call | solution.py:1268

commit v7 on v6

--- a/solution.py
+++ b/solution.py
@@ -834,30 +834,27 @@
         partition = partition + stat_all[i]
     scale = weight / partition
 
-    lane_parts = [pl.ds(0, half - 128), pl.ds(half - 128, 128)]
+    lane_parts = [pl.ds(0, 128), pl.ds(128, half - 128)]
 
     def delta_copy(p):
         here = lane_parts[p]
         return copy(delta.at[0, :, here], delta.at[1, :, here], es.at[0], (cr, er)[p].at[0], over_y, v)
 
-    for n in range(steps):
-        for k in range(2):
-            i = 2 * n + k
-            span = pl.ds(i * rows, rows)
-            by_row = jnp.transpose(jnp.broadcast_to(scale[i:i + 1, :], (rows, rows)))
-            factor = jnp.concatenate([by_row] * (half // rows), axis=1)
-            delta[0, span, :] = (expo[span, :] * factor - logits[span, :]).astype(bf16)
-    for p in range(2):
-        delta_copy(p).start()
-
     chunks = range(half // 128)
 
     def chunk_of_delta(n):
         here = pl.ds(n * 128, 128)
         return copy(delta.at[0, :, here], d_end.at[:, here], zs.at[0], zr.at[n], near_end * ny + y, v)
 
+    by_row = [jnp.transpose(jnp.broadcast_to(scale[i:i + 1, :], (rows, rows))) for i in range(group)]
     for n in chunks:
+        here = pl.ds(n * 128, 128)
+        for i in range(group):
+            span = pl.ds(i * rows, rows)
+            delta[0, span, here] = (expo[span, here] * by_row[i] - logits[span, here]).astype(bf16)
         pl.when(at_end)(lambda: chunk_of_delta(n).start())
+        if n in (0, half // 128 - 1):
+            delta_copy(min(n, 1)).start()
 
     targets = [jnp.where(at_end, far, across), jnp.where(at_end, across, near), jnp.where(at_end, near_end, far), z]
     top = y * shift

time: 100 us -> 99.7 us (level)
  Pallas kernels: 99.4 us -> 98.3 us
    pallas_call x1, Pallas kernels: 97.7 us -> 96.6 us  [plane_local(): pl.pallas_call(plane_kernel, out_shape=(vm((cols, entries), f32), vm((row...]
where the time goes in v7:
time: 99.7 us; the launch traced here: 99.1 us
  Pallas kernels  98.3 us (99%)
    pallas_call x1, Pallas kernels, plane_local(): pl.pallas_call(plane_kernel, out_shape=(vm((cols, entries), f32), vm((row...  96.6 us

profile of v7, /device:TPU:0, one launch (start us, length us, event | category | flops | bytes accessed | tf_op | source)
XLA Modules:
  0.0 99.1 jit_solution(15584240026565527210)
XLA Ops:
  0.6 96.6 %shard_map.67 = (f32[448,768]{1,0:T(8,128)S(1)}, f32[128,3584]{1,0:T(8,128)S(1)}, f32[8,128]{1,0:T(8,128)S(1)}) custom-call(bf16[128,3584]{1,0:T(8,128)(2,1)} %h_in.1, bf16[448,768]{1,0:T(8,128)(2,1)} %bitcast.5, s32[1,128]{1,0:T(1,128)} %bitcast.6, s32[1,128]{1,0:T(1,128)} %bitcast.7), custom_call_target="tpu_custom_call" | custom-call | tf_op jit(solution)/shard_map/pallas_call | solution.py:1251
  97.2 1.7 %shard_map.68 = (f32[448,768]{1,0:T(8,128)}, f32[128,3584]{1,0:T(8,128)}, f32[1,1]{1,0:T(1,128)}) custom-call(f32[448,768]{1,0:T(8,128)S(1)} %get-tuple-element.9.head_in, f32[128,3584]{1,0:T(8,128)S(1)} %get-tuple-element.10.hid_in, f32[8,128]{1,0:T(8,128)S(1)} %get-tuple-element.11.loss_in), custom_call_target="tpu_custom_call" | custom-call | tf_op jit(solution)/shard_map/pallas_call | solution.py:1265

commit v8 on v7

--- a/solution.py
+++ b/solution.py
@@ -709,9 +709,9 @@
         pl.when(has_down)(lambda: w_z(i, h, False).start())
     send_out(0, 0)
 
-    def w_slab(zz, onward, which=(0, 1)):
+    def w_slab(zz, onward, which=(0, 1), halves=(0, 1)):
         for k in which:
-            for h in range(2):
+            for h in halves:
                 i = zz * ny + flip(y, k)
                 w_got(i, h)
                 if onward:
@@ -779,12 +779,15 @@
     pl.when(at_end)(lambda: w_slab(slabs[3], False, (0,)))
     for n in range(steps):
         logits[n * step:(n + 1) * step, :] += scores(n, slabs[3], y * (slab - early), early)
-    pl.when(at_end)(lambda: w_slab(slabs[3], False, (1,)))
+    pl.when(at_end)(lambda: w_slab(slabs[3], False, (1,), (0,)))
+    for n in range(steps):
+        logits[n * step:(n + 1) * step, :] += scores(n, slabs[3], (1 - y) * early, 128)
+    pl.when(at_end)(lambda: w_slab(slabs[3], False, (1,), (1,)))
 
     sums = jnp.zeros((8, rows), f32)
     for n in range(steps):
         span = pl.ds(n * step, step)
-        capped = softcap * jnp.tanh((logits[span, :] + scores(n, slabs[3], (1 - y) * early, slab - early)) * (1.0 / softcap))
+        capped = softcap * jnp.tanh((logits[span, :] + scores(n, slabs[3], (1 - y) * early + 128, slab - early - 128)) * (1.0 / softcap))
         raised = jnp.exp(capped)
         logits[span, :] = capped
         expo[span, :] = raised
@@ -834,10 +837,11 @@
         partition = partition + stat_all[i]
     scale = weight / partition
 
-    lane_parts = [pl.ds(0, 128), pl.ds(128, half - 128)]
+    lane_parts = [pl.ds(n * 128, 128) for n in range(half // 128)]
+    over_parts = [pl.ds(0, 128), pl.ds(128, half - 128)]
 
     def delta_copy(p):
-        here = lane_parts[p]
+        here = over_parts[p]
         return copy(delta.at[0, :, here], delta.at[1, :, here], es.at[0], (cr, er)[p].at[0], over_y, v)
 
     chunks = range(half // 128)
@@ -914,17 +918,20 @@
             grad_own[0, :, first:first + 128] += over_tokens(h_end[:, 2 * win:3 * win], right)
 
     def head_part(k, p):
-        here = lane_parts[p]
+        here = over_parts[p]
         share = over_tokens(h_all[:, window(targets[k])], delta[1, :, here])
+        which = chunks[1:] if p else chunks[:1]
         if k:
             grad_send[k, 1, :, here] = share.astype(bf16)
-            pl.when(at_end)(lambda: relay_copy(1, p).start())
-            pl.when(inside)(lambda: part_copy(k, p).start())
+            for q in which:
+                pl.when(at_end)(lambda: relay_copy(1, q).start())
+                pl.when(inside)(lambda: part_copy(k, q).start())
         else:
             @pl.when(at_end)
             def _():
                 grad_send[k, 1, :, here] = share.astype(bf16)
-                relay_copy(0, p).start()
+                for q in which:
+                    relay_copy(0, q).start()
 
             @pl.when(inside)
             def _():
@@ -1137,8 +1144,10 @@
     copy(core_in, core_in, ds.at[0], wr.at[0, 0], b, over_core).wait_send()
     one_sum(4)
     two_sum(1)
-    relay(2, 0, 1)
-    relay(0, 1, 1)
+    for p in chunks[1:]:
+        relay(2, 0, p)
+    for p in chunks[1:]:
+        relay(0, 1, p)
     for g in range(5, count):
         one_sum(g)
     two_sum(2)
@@ -1244,7 +1253,7 @@
     sems = [
         dma((5,)), dma((1,)), dma((group,)), dma((2,)), dma((8, 2)), dma((1,)),
         dma((1,)), dma((1,)), dma((1,)), dma((1,)), dma((1,)), dma((1,)), dma((1,)), dma((1,)),
-        dma((1,)), dma((1,)), dma((1,)), dma((nz, 2)), dma((2, 2)), dma((1,)), dma((half // 128,)), dma((1,)), dma((group,)),
+        dma((1,)), dma((1,)), dma((1,)), dma((nz, 2)), dma((2, half // 128)), dma((1,)), dma((half // 128,)), dma((1,)), dma((group,)),
         dma((1,)), dma((1,)), dma((count,)), dma((1,)),
     ]
     whole = pl.BlockSpec(memory_space=vm)
@@ -1282,7 +1291,7 @@
     entries, cols = head_weight.shape
     fits = nb == 8 and nv == 4 and rows == 128 and width % 256 == 0 and width >= 3072
     fits = fits and len(column_groups(width)) <= 8
-    return fits and entries % 256 == 0 and entries >= 512 and cols % 32 == 0 and (2 * cols) % 128 == 0
+    return fits and cols >= 256 and entries % 256 == 0 and entries >= 512 and cols % 32 == 0 and (2 * cols) % 128 == 0
 
 
 def device(nb, nv, *arrays):

time: 99.7 us -> 99.7 us (level)
  no operation moved by 1% of the time
where the time goes in v8:
time: 99.7 us; the launch traced here: 99.1 us
  Pallas kernels  98.3 us (99%)
    pallas_call x1, Pallas kernels, plane_local(): pl.pallas_call(plane_kernel, out_shape=(vm((cols, entries), f32), vm((row...  96.6 us

profile of v8, /device:TPU:0, one launch (start us, length us, event | category | flops | bytes accessed | tf_op | source)
XLA Modules:
  0.0 99.1 jit_solution(6133661670837630378)
XLA Ops:
  0.6 96.6 %shard_map.67 = (f32[448,768]{1,0:T(8,128)S(1)}, f32[128,3584]{1,0:T(8,128)S(1)}, f32[8,128]{1,0:T(8,128)S(1)}) custom-call(bf16[128,3584]{1,0:T(8,128)(2,1)} %h_in.1, bf16[448,768]{1,0:T(8,128)(2,1)} %bitcast.5, s32[1,128]{1,0:T(1,128)} %bitcast.6, s32[1,128]{1,0:T(1,128)} %bitcast.7), custom_call_target="tpu_custom_call" | custom-call | tf_op jit(solution)/shard_map/pallas_call | solution.py:1260
  97.2 1.7 %shard_map.68 = (f32[448,768]{1,0:T(8,128)}, f32[128,3584]{1,0:T(8,128)}, f32[1,1]{1,0:T(1,128)}) custom-call(f32[448,768]{1,0:T(8,128)S(1)} %get-tuple-element.9.head_in, f32[128,3584]{1,0:T(8,128)S(1)} %get-tuple-element.10.hid_in, f32[8,128]{1,0:T(8,128)S(1)} %get-tuple-element.11.loss_in), custom_call_target="tpu_custom_call" | custom-call | tf_op jit(solution)/shard_map/pallas_call | solution.py:1274
